TPU v7x, 8 devices: a whole 2x2x1 slice. The times are simulated.
8 devices in a mesh: my: 4 (over z, y, x), mx: 2 (over core).
Axes of the slice: x: 2, y: 2, z: 1, core: 2. Of those that a mesh axis runs over, the one named last changes fastest.
Arguments:
- x_in: bfloat16 [384, 5120], P(None, 'mx')
- seq_lens: int32 [384], P('mx')
- gain_attn: bfloat16 [5120], P('mx')
- gain_mlp: bfloat16 [5120], P('mx')
- w_q: bfloat16 [5120, 5120], P('mx', 'my')
- b_q: bfloat16 [5120], P('my')
- w_k: bfloat16 [5120, 1024], P('mx', 'my')
- b_k: bfloat16 [1024], P('my')
- w_v: bfloat16 [5120, 1024], P('mx', 'my')
- b_v: bfloat16 [1024], P('my')
- w_o: bfloat16 [5120, 5120], P('my', 'mx')
- w_gate: bfloat16 [5120, 13824], P('mx', 'my')
- w_up: bfloat16 [5120, 13824], P('mx', 'my')
- w_down: bfloat16 [13824, 5120], P('my', 'mx')
- k_cache: bfloat16 [384, 256, 8, 128], P('mx', None, 'my')
- v_cache: bfloat16 [384, 256, 8, 128], P('mx', None, 'my')
Outputs:
- output 1: bfloat16 [384, 5120], P(None, 'mx')
- output 2: bfloat16 [384, 256, 8, 128], P('mx', None, 'my')
- output 3: bfloat16 [384, 256, 8, 128], P('mx', None, 'my')
All inputs are finite; a program needn't handle non-finite values.
Results may differ from a plain program's by a relative error of at most 0.0165212.
Values are sent between devices in bfloat16 or wider.
A program may use at most 1 GiB of HBM per device.

v0:
```python
import jax
import jax.numpy as jnp
from jax import lax
from jax.sharding import PartitionSpec as P

HEAD = 128
NORM_EPS = 1e-6
ROPE_THETA = 1000000.0


def apply_rotary(vectors, positions):
    half_dim = HEAD // 2
    inv_freq = ROPE_THETA ** (-2.0 * jnp.arange(half_dim, dtype=jnp.float32) / HEAD)
    angles = positions.astype(jnp.float32)[:, None, None] * inv_freq
    cos_tab = jnp.cos(angles)
    sin_tab = jnp.sin(angles)
    lower_half = vectors[..., :half_dim]
    upper_half = vectors[..., half_dim:]
    return jnp.concatenate([lower_half * cos_tab - upper_half * sin_tab, upper_half * cos_tab + lower_half * sin_tab], axis=-1)


def attend_local(q_rot, k_cache_out, v_cache_out, seq_lens):
    row_count, seq_len, kv_heads, _ = k_cache_out.shape
    q_heads = q_rot.shape[1]
    q_grouped = q_rot.reshape(row_count, kv_heads, q_heads // kv_heads, HEAD)
    scores = jnp.einsum("bkgd,bskd->bkgs", q_grouped, k_cache_out, preferred_element_type=jnp.float32) * HEAD ** -0.5
    visible = (jnp.arange(seq_len)[None, :] <= seq_lens[:, None])[:, None, None, :]
    scores = jnp.where(visible, scores, -jnp.inf)
    weights = jnp.exp(scores - jnp.max(scores, axis=-1, keepdims=True))
    weight_sum = jnp.sum(weights, axis=-1, keepdims=True)
    weighted = jnp.einsum("bkgs,bskd->bkgd", weights.astype(jnp.bfloat16), v_cache_out, preferred_element_type=jnp.float32)
    return (weighted / weight_sum).astype(jnp.bfloat16).reshape(row_count, q_heads * HEAD)


def solution(mesh):
    mx_size = mesh.shape["mx"]
    act_spec = P(None, "mx")
    cache_spec = P("mx", None, "my", None)
    in_specs = (act_spec, P("mx"), P("mx"), P("mx"), P("mx", "my"), P("my"), P("mx", "my"), P("my"), P("mx", "my"), P("my"), P("my", "mx"), P("mx", "my"), P("mx", "my"), P("my", "mx"), cache_spec, cache_spec)
    out_specs = (act_spec, cache_spec, cache_spec)

    def local_layer(x_in, seq_lens, gain_attn, gain_mlp, w_q, b_q, w_k, b_k, w_v, b_v, w_o, w_gate, w_up, w_down, k_cache, v_cache):
        hidden = x_in.shape[1] * mx_size
        x_f32 = x_in.astype(jnp.float32)
        attn_sq = lax.psum(jnp.sum(x_f32 * x_f32, axis=1, keepdims=True), "mx")
        normed = (x_f32 * lax.rsqrt(attn_sq / hidden + NORM_EPS) * gain_attn.astype(jnp.float32)).astype(jnp.bfloat16)
        q_cols = w_q.shape[1]
        kv_cols = w_k.shape[1]
        partials = jnp.concatenate([
            jnp.dot(normed, w_q, preferred_element_type=jnp.float32).astype(jnp.bfloat16),
            jnp.dot(normed, w_k, preferred_element_type=jnp.float32).astype(jnp.bfloat16),
            jnp.dot(normed, w_v, preferred_element_type=jnp.float32).astype(jnp.bfloat16),
        ], axis=1)
        projected = lax.psum_scatter(partials, "mx", scatter_dimension=0, tiled=True).astype(jnp.float32)
        row_count = projected.shape[0]
        kv_heads = kv_cols // HEAD
        q_vals = projected[:, :q_cols] + b_q.astype(jnp.float32)
        k_vals = projected[:, q_cols:q_cols + kv_cols] + b_k.astype(jnp.float32)
        v_vals = projected[:, q_cols + kv_cols:] + b_v.astype(jnp.float32)
        q_rot = apply_rotary(q_vals.reshape(row_count, q_cols // HEAD, HEAD), seq_lens).astype(jnp.bfloat16)
        k_rot = apply_rotary(k_vals.reshape(row_count, kv_heads, HEAD), seq_lens).astype(jnp.bfloat16)
        v_new = v_vals.reshape(row_count, kv_heads, HEAD).astype(jnp.bfloat16)
        at_slot = (jnp.arange(k_cache.shape[1])[None, :] == seq_lens[:, None])[:, :, None, None]
        k_cache_out = jnp.where(at_slot, k_rot[:, None], k_cache)
        v_cache_out = jnp.where(at_slot, v_new[:, None], v_cache)
        attn_rows = attend_local(q_rot, k_cache_out, v_cache_out, seq_lens)
        attn_all = lax.all_gather(attn_rows, "mx", axis=0, tiled=True)
        attn_proj = lax.psum(jnp.dot(attn_all, w_o, preferred_element_type=jnp.float32).astype(jnp.bfloat16), "my")
        x_mid = (x_f32 + attn_proj.astype(jnp.float32)).astype(jnp.bfloat16)
        mid_f32 = x_mid.astype(jnp.float32)
        mlp_sq = lax.psum(jnp.sum(mid_f32 * mid_f32, axis=1, keepdims=True), "mx")
        normed_mlp = (mid_f32 * lax.rsqrt(mlp_sq / hidden + NORM_EPS) * gain_mlp.astype(jnp.float32)).astype(jnp.bfloat16)
        ff_cols = w_gate.shape[1]
        gate_up = lax.psum(jnp.concatenate([
            jnp.dot(normed_mlp, w_gate, preferred_element_type=jnp.float32).astype(jnp.bfloat16),
            jnp.dot(normed_mlp, w_up, preferred_element_type=jnp.float32).astype(jnp.bfloat16),
        ], axis=1), "mx").astype(jnp.float32)
        hidden_act = (jax.nn.silu(gate_up[:, :ff_cols]) * gate_up[:, ff_cols:]).astype(jnp.bfloat16)
        down_proj = lax.psum(jnp.dot(hidden_act, w_down, preferred_element_type=jnp.float32).astype(jnp.bfloat16), "my")
        x_out = (mid_f32 + down_proj.astype(jnp.float32)).astype(jnp.bfloat16)
        return x_out, k_cache_out, v_cache_out

    return jax.shard_map(local_layer, mesh=mesh, in_specs=in_specs, out_specs=out_specs, check_vma=False)
```

profile of v0, /device:TPU:0, one launch (start us, length us, event | category | flops | bytes accessed | tf_op | source)
XLA Modules:
  0.0 350.6 jit_solution(10786160470866159356)
XLA Ops:
  7.2 2.1 fusion.5
  9.3 3.0 psum.35
  13.1 2.4 convolution_convert_fusion.6
  16.3 2.1 copy-done.12
  18.4 2.8 convolution_convert_fusion.4
  25.1 5.7 %reduce-scatter.2.cloned.1.call-done = bf16[192,1792]{1,0:T(8,128)(2,1)} async-done(((bf16[384,1792]{1,0:T(8,128)(2,1)}), bf16[192,1792]{1,0:T(8,128)(2,1)}) %reduce-scatter.2.cloned.1.call-update) | async-done | bytes 688144 | tf_op jit(solution)/shard_map/reduce_scatter | solution.py:54
  39.0 2.5 copy.36
  43.1 68.6 %broadcast_select_fusion = (bf16[192,256,2,128]{3,2,1,0:T(2,128)(2,1)}, bf16[192,256,2,128]{3,2,1,0:T(2,128)(2,1)}) fusion(bf16[192,256,2,128]{3,2,1,0:T(2,128)(2,1)} %param.31, pred[192,256]{1,0:T(8,128)(4,1)S(1)} %copy-done.8, bf16[192,2,128]{2,1,0:T(2,128)(2,1)S(1)} %copy-done.7, bf16[192,256,2,128]{3,2,1,0:T(2,128)(2,1)} %param.30, ...), kind=kLoop, calls=%fused_computation | loop fusion | flops 25165824 | bytes 100909056 | tf_op jit(solution)/shard_map/jit(_where)/select_n | solution.py:65
  111.6 16.7 %fusion.13 = (f32[192,2,5]{2,1,0:T(2,128)S(1)}, f32[192,2,5,256]{3,2,1,0:T(8,128)}) fusion(pred[192,256]{1,0:T(8,128)(4,1)S(1)} %get-tuple-element.15, bf16[192,256,2,128]{3,2,1,0:T(2,128)(2,1)} %get-tuple-element.12, bf16[192,2,5,64]{3,2,1,0:T(8,128)(2,1)S(1)} %copy.37, bf16[192,2,5,64]{3,2,1,0:T(8,128)(2,1)} %copy.36), kind=kOutput, calls=%fused_computation.30 | convolution fusion | flops 128284800 | bytes 27680256 | tf_op jit(solution)/shard_map/bkgd,bskd->bkgs/dot_general | solution.py:26
  128.3 3.0 fusion.16
  131.4 12.3 %divide_convert_fusion = bf16[192,2,5,128]{3,2,1,0:T(8,128)(2,1)} fusion(f32[192,2,5]{2,1,0:T(2,128)S(1)} %fusion.16, bf16[192,256,2,128]{3,2,1,0:T(2,128)(2,1)} %get-tuple-element.11, f32[192,2,5,256]{3,2,1,0:T(8,128)S(1)} %copy-done.2, f32[192,2,5]{2,1,0:T(2,128)S(1)} %get-tuple-element.17, pred[192,256]{1,0:T(8,128)(4,1)S(1)} %get-tuple-element.15), kind=kOutput, calls=%fused_computation.34 | convolution fusion | flops 128286720 | bytes 27687936 | tf_op jit(solution)/shard_map/bkgs,bskd->bkgd/dot_general | solution.py:31
  145.5 2.5 all_gather.3
  148.0 6.7 %convolution_convert_fusion.2 = bf16[384,2560]{1,0:T(8,128)(2,1)} fusion(bf16[384,1280]{1,0:T(8,128)(2,1)S(1)} %all_gather.3, bf16[1280,2560]{1,0:T(8,128)(2,1)} %param.26), kind=kOutput, calls=%fused_computation.17 | convolution fusion | flops 2517565440 | bytes 9502720 | tf_op jit(solution)/shard_map/dot_general | solution.py:68
  154.8 56.9 %all-reduce.4.cloned.1.call-done = bf16[384,2560]{1,0:T(8,128)(2,1)} async-done(((bf16[384,2560]{1,0:T(8,128)(2,1)}), bf16[384,2560]{1,0:T(8,128)(2,1)}) %all-reduce.4.cloned.1.call-update) | async-done | bytes 1966096 | tf_op jit(solution)/shard_map/psum | solution.py:68
  211.7 3.6 %fusion.9 = (f32[384]{0:T(512)S(1)}, bf16[384,2560]{1,0:T(8,128)(2,1)}) fusion(bf16[384,2560]{1,0:T(8,128)(2,1)} %all-reduce.4.cloned.1.call-done, bf16[384,2560]{1,0:T(8,128)(2,1)S(1)} %copy-done.3), kind=kLoop, calls=%fused_computation.23 | loop fusion | flops 6880896 | bytes 5899776 | tf_op jit(solution)/shard_map/reduce_sum | solution.py:71
  215.3 2.4 psum.37
  217.8 11.9 %convolution_convert_fusion = bf16[384,3456]{1,0:T(8,128)(2,1)S(1)} fusion(bf16[2560,3456]{1,0:T(8,128)(2,1)} %param.28, bf16[384,2560]{1,0:T(8,128)(2,1)} %get-tuple-element.4, f32[2560]{0:T(1024)S(1)} %convert_element_type.115, f32[384]{0:T(512)S(1)} %rsqrt_reduce_fusion), kind=kOutput, calls=%fused_computation.12 | convolution fusion | flops 6800031744 | bytes 22326784 | tf_op jit(solution)/shard_map/dot_general | solution.py:76
  229.7 11.2 %convolution_convert_fusion.1 = bf16[384,3456]{1,0:T(8,128)(2,1)S(1)} fusion(bf16[2560,3456]{1,0:T(8,128)(2,1)} %param.27, bf16[384,2560]{1,0:T(8,128)(2,1)S(1)} %copy-done.4, f32[2560]{0:T(1024)S(1)} %convert_element_type.115, f32[384]{0:T(512)S(1)} %rsqrt_reduce_fusion), kind=kOutput, calls=%fused_computation.13 | convolution fusion | flops 6800031744 | bytes 22326784 | tf_op jit(solution)/shard_map/dot_general | solution.py:75
  240.9 2.7 pad_maximum_fusion
  243.7 23.1 %all-reduce.6.cloned.1.call-done = bf16[384,6912]{1,0:T(8,128)(2,1)} async-done(((bf16[384,6912]{1,0:T(8,128)(2,1)}), bf16[384,6912]{1,0:T(8,128)(2,1)}) %all-reduce.6.cloned.1.call-update) | async-done | bytes 5308432 | tf_op jit(solution)/shard_map/psum | solution.py:74
  266.8 3.2 convert_element_type.119
  270.0 13.8 %convolution_convert_fusion.3 = bf16[384,2560]{1,0:T(8,128)(2,1)} fusion(bf16[3456,2560]{1,0:T(8,128)(2,1)} %param.29, f32[384,6912]{1,0:T(8,128)S(1)} %convert_element_type.119), kind=kOutput, calls=%fused_computation.18 | convolution fusion | flops 6803718144 | bytes 30277632 | tf_op jit(solution)/shard_map/dot_general | solution.py:79
  283.9 57.0 %all-reduce.8.cloned.1.call-done = bf16[384,2560]{1,0:T(8,128)(2,1)} async-done(((bf16[384,2560]{1,0:T(8,128)(2,1)}), bf16[384,2560]{1,0:T(8,128)(2,1)}) %all-reduce.8.cloned.1.call-update) | async-done | bytes 1966096 | tf_op jit(solution)/shard_map/psum | solution.py:79
  340.8 3.3 fusion.12
  (68 shorter events, 17.1 us)
Async XLA Ops:
  7.2 5.9 %copy-start = (bf16[2560,256]{1,0:T(8,128)(2,1)S(1)}, bf16[2560,256]{1,0:T(8,128)(2,1)}, u32[]{:S(2)}) copy-start(bf16[2560,256]{1,0:T(8,128)(2,1)} %param.22) | copy-start | bytes 3932164
  7.2 23.6 %reduce-scatter.2.cloned.1.call-start = ((), (), s32[]{:S(2)}) async-start(), calls=%async_computation.1 | async-start | bytes 2064384 | tf_op jit(solution)/shard_map/reduce_scatter | solution.py:54
  13.1 2.4 copy-start.3
  13.1 2.5 copy-start.13
  15.6 2.9 copy-start.12
  21.2 1.3 copy-start.14
  21.2 1.3 copy-start.15
  21.2 1.3 copy-start.10
  21.2 1.3 copy-start.11
  22.5 189.2 %all-reduce.4.cloned.1.call-start = ((), (), s32[]{:S(2)}) async-start(), calls=%async_computation.2 | async-start | bytes 3932160 | tf_op jit(solution)/shard_map/psum | solution.py:68
  22.9 9.1 %copy-start.5 = (f32[192,64]{0,1:T(8,128)}, f32[192,64]{0,1:T(8,128)S(1)}, u32[]{:S(2)}) copy-start(f32[192,64]{0,1:T(8,128)S(1)} %get-tuple-element.13) | copy-start | bytes 147460
  22.9 9.1 %copy-start.6 = (f32[192,64]{0,1:T(8,128)}, f32[192,64]{0,1:T(8,128)S(1)}, u32[]{:S(2)}) copy-start(f32[192,64]{0,1:T(8,128)S(1)} %get-tuple-element.14) | copy-start | bytes 147460
  37.4 5.7 %copy-start.7 = (bf16[192,2,128]{2,1,0:T(2,128)(2,1)S(1)}, bf16[192,2,128]{2,1,0:T(2,128)(2,1)}, u32[]{:S(2)}) copy-start(bf16[192,2,128]{2,1,0:T(2,128)(2,1)} %convert_element_type.109) | copy-start | bytes 294916
  37.4 5.7 %copy-start.8 = (pred[192,256]{1,0:T(8,128)(4,1)S(1)}, pred[192,256]{1,0:T(8,128)(4,1)}, u32[]{:S(2)}) copy-start(pred[192,256]{1,0:T(8,128)(4,1)} %get-tuple-element.16) | copy-start | bytes 147460
  128.3 3.0 copy-start.2
  148.0 6.8 %copy-start.9 = (bf16[2560]{0:T(1024)(128)(2,1)S(1)}, bf16[2560]{0:T(1024)(128)(2,1)}, u32[]{:S(2)}) copy-start(bf16[2560]{0:T(1024)(128)(2,1)} %param.19) | copy-start | bytes 15364
  154.7 112.1 %all-reduce.6.cloned.1.call-start = ((), (), s32[]{:S(2)}) async-start(), calls=%async_computation.3 | async-start | bytes 10616832 | tf_op jit(solution)/shard_map/psum | solution.py:74
  217.8 11.9 %copy-start.4 = (bf16[384,2560]{1,0:T(8,128)(2,1)S(1)}, bf16[384,2560]{1,0:T(8,128)(2,1)}, u32[]{:S(2)}) copy-start(bf16[384,2560]{1,0:T(8,128)(2,1)} %get-tuple-element.4) | copy-start | bytes 5898244
  243.6 97.2 %all-reduce.8.cloned.1.call-start = ((), (), s32[]{:S(2)}) async-start(), calls=%async_computation.4 | async-start | bytes 3932160 | tf_op jit(solution)/shard_map/psum | solution.py:79
  283.8 60.3 %copy-start.1 = (bf16[2560,256]{1,0:T(8,128)(2,1)S(1)}, bf16[2560,256]{1,0:T(8,128)(2,1)}, u32[]{:S(2)}) copy-start(bf16[2560,256]{1,0:T(8,128)(2,1)} %param.22) | copy-start | bytes 3932164
Sparse Core Ops, SparseCore 0:
  22.6 8.2 reduce-scatter.1
  154.8 56.7 all-reduce.3
  243.7 23.0 all-reduce.5
  284.0 56.8 all-reduce.7
where the time goes:
time: 351 us
  waiting for transfers between devices  143 us (41%)
  other arithmetic  95.2 us (27%)
  matrix products  78.6 us (22%)
  between operations  14.1 us (4%)
  local copies, waits for them, and re-layouts  12 us (3%)
  blocking collectives  7.94 us (2%)
    select_n x1, other arithmetic, local_layer(): v_cache_out = jnp.where(at_slot, v_new[:, None], v_cache)  68.6 us
    psum x1, waiting for transfers between devices, local_layer(): lax.psum(jnp.dot(hidden_act, w_down, preferred_element_type=jnp.float32)....  57 us
    psum x1, waiting for transfers between devices, local_layer(): lax.psum(jnp.dot(attn_all, w_o, preferred_element_type=jnp.float32).astyp...  56.9 us
    psum x1, waiting for transfers between devices, local_layer(): lax.psum(jnp.concatenate([jnp.dot(normed_mlp, w_gate, preferred_element_t...  23.1 us
    dot_general x1, matrix products, attend_local(): jnp.einsum('bkgd,bskd->bkgs', q_grouped, k_cache_out, preferred_element_t...  16.7 us
    dot_general x1, matrix products, local_layer(): jnp.dot(hidden_act, w_down, preferred_element_type=jnp.float32)  13.8 us
    dot_general x1, matrix products, attend_local(): jnp.einsum('bkgs,bskd->bkgd', weights.astype(jnp.bfloat16), v_cache_out,...  12.3 us
    dot_general x1, matrix products, local_layer(): jnp.dot(normed_mlp, w_up, preferred_element_type=jnp.float32)  11.9 us
  transfers between devices with their start and end apart: 4, of which 4 were waited for; matrix products, arithmetic and copies ran while one was open for 1% of the time, Pallas kernels for 0%

commit v1 on v0

v1 whole, which is shorter than its diff:
```python
import jax
import jax.numpy as jnp
from jax import lax
from jax.experimental import pallas as pl
from jax.experimental.pallas import tpu as pltpu
from jax.sharding import PartitionSpec as P

HEAD = 128
NORM_EPS = 1e-6
ROPE_THETA = 1000000.0
SLOT_ROWS = 8
SLOTS = 8
AHEAD = 6
PAD_HEADS = 16


def attend_kernel(lens, q_ref, kn_ref, vn_ref, kc, vc, ko, vo, out_ref, kbuf, vbuf, qs, os, sems):
    rows = q_ref.shape[0]
    heads = q_ref.shape[1] // HEAD
    flat = kbuf.shape[2]
    blocks = rows // SLOT_ROWS

    def moves(block, slot, inward):
        part = pl.ds(block * SLOT_ROWS, SLOT_ROWS)
        if inward:
            return (pltpu.make_async_copy(kc.at[part], kbuf.at[slot], sems.at[0, slot]),
                    pltpu.make_async_copy(vc.at[part], vbuf.at[slot], sems.at[1, slot]))
        return (pltpu.make_async_copy(kbuf.at[slot], ko.at[part], sems.at[2, slot]),
                pltpu.make_async_copy(vbuf.at[slot], vo.at[part], sems.at[3, slot]))

    for block in range(AHEAD):
        for move in moves(block, block, True):
            move.start()
    qs[...] = jnp.zeros_like(qs)

    tile_row = lax.broadcasted_iota(jnp.int32, (PAD_HEADS, HEAD), 0)
    pair_row = lax.broadcasted_iota(jnp.int32, (2 * PAD_HEADS, flat), 0)
    col = lax.broadcasted_iota(jnp.int32, (2 * PAD_HEADS, flat), 1)
    second = pair_row >= PAD_HEADS
    head_of_row = jnp.where(pair_row % PAD_HEADS >= heads // 2, 1, 0)
    col_pos = jnp.where(col % 2 == head_of_row, col // 2, jnp.int32(1 << 20))
    zeros = jnp.zeros((PAD_HEADS, HEAD), jnp.bfloat16)

    def put_row(buf, slot, j, pos, new8):
        base = pl.multiple_of((2 * pos) // 16 * 16, 16)
        off = 2 * pos - base
        tile = buf[slot, j, pl.ds(base, 16), :]
        first = jnp.broadcast_to(new8[j:j + 1, :HEAD], (16, HEAD)).astype(jnp.bfloat16)
        other = jnp.broadcast_to(new8[j:j + 1, HEAD:], (16, HEAD)).astype(jnp.bfloat16)
        tile = jnp.where(tile_row == off, first, jnp.where(tile_row == off + 1, other, tile))
        buf[slot, j, pl.ds(base, 16), :] = tile

    @pl.loop(0, blocks // 2)
    def _(step):
        for half in range(2):
            block = step * 2 + half
            slot = lax.rem(block, SLOTS)
            for move in moves(block, slot, True):
                move.wait()
            rows8 = pl.ds(pl.multiple_of(block * SLOT_ROWS, SLOT_ROWS), SLOT_ROWS)
            kn8, vn8 = kn_ref[rows8, :], vn_ref[rows8, :]
            for h in range(heads):
                qs[pl.ds(h, SLOT_ROWS, stride=PAD_HEADS), :] = q_ref[rows8, h * HEAD:(h + 1) * HEAD]
            for j in range(SLOT_ROWS):
                b = block * SLOT_ROWS + j
                put_row(kbuf, slot, j, lens[b], kn8)
                put_row(vbuf, slot, j, lens[b], vn8)
            pairs = range(0, SLOT_ROWS, 2)
            scores = []
            for j in pairs:
                q0 = qs[j * PAD_HEADS:(j + 1) * PAD_HEADS, :].astype(jnp.bfloat16)
                q1 = qs[(j + 1) * PAD_HEADS:(j + 2) * PAD_HEADS, :].astype(jnp.bfloat16)
                qp = jnp.concatenate([jnp.concatenate([q0, zeros], axis=1), jnp.concatenate([zeros, q1], axis=1)], axis=0)
                kp = jnp.concatenate([kbuf[slot, j], kbuf[slot, j + 1]], axis=1)
                scores.append(lax.dot_general(qp, kp, (((1,), (1,)), ((), ())), preferred_element_type=jnp.float32))
            probs = []
            for i, j in enumerate(pairs):
                b = block * SLOT_ROWS + j
                limit = jnp.where(second, lens[b + 1], lens[b])
                s = jnp.where(col_pos <= limit, scores[i] * HEAD ** -0.5, -jnp.inf)
                e = jnp.exp(s - jnp.max(s, axis=-1, keepdims=True))
                probs.append((e.astype(jnp.bfloat16), jnp.sum(e, axis=-1, keepdims=True)))
            for i, j in enumerate(pairs):
                e, total = probs[i]
                vp = jnp.concatenate([vbuf[slot, j], vbuf[slot, j + 1]], axis=1)
                o = jnp.dot(e, vp, preferred_element_type=jnp.float32)
                at = (half * SLOT_ROWS + j) * PAD_HEADS
                os[at:at + PAD_HEADS, :] = o[:PAD_HEADS, :HEAD] / total[:PAD_HEADS]
                os[at + PAD_HEADS:at + 2 * PAD_HEADS, :] = o[PAD_HEADS:, HEAD:] / total[PAD_HEADS:]
            for move in moves(block, slot, False):
                move.start()

            @pl.when(block + AHEAD < blocks)
            def _():
                later = lax.rem(block + AHEAD, SLOTS)

                @pl.when(block + AHEAD >= SLOTS)
                def _():
                    for move in moves(block + AHEAD - SLOTS, later, False):
                        move.wait()
                for move in moves(block + AHEAD, later, True):
                    move.start()
        for h in range(heads):
            out_ref[pl.ds(pl.multiple_of(step * 16, 16), 16), h * HEAD:(h + 1) * HEAD] = os[pl.ds(h, 16, stride=PAD_HEADS), :].astype(jnp.bfloat16)

    for block in range(blocks - SLOTS, blocks):
        for move in moves(block, block % SLOTS, False):
            move.wait()


def attend(lens, q, k_new, v_new, k_cache, v_cache):
    rows, seq, kv, _ = k_cache.shape
    flat = seq * kv
    kc = k_cache.reshape(rows, flat, HEAD)
    vc = v_cache.reshape(rows, flat, HEAD)
    whole = pl.BlockSpec(memory_space=pltpu.VMEM)
    hbm = pl.BlockSpec(memory_space=pltpu.HBM)
    ko, vo, out = pl.pallas_call(
        attend_kernel,
        out_shape=(jax.ShapeDtypeStruct(kc.shape, kc.dtype), jax.ShapeDtypeStruct(vc.shape, vc.dtype), jax.ShapeDtypeStruct(q.shape, jnp.bfloat16)),
        in_specs=[pl.BlockSpec(memory_space=pltpu.SMEM), whole, whole, whole, hbm, hbm],
        out_specs=(hbm, hbm, whole),
        scratch_shapes=[
            pltpu.VMEM((SLOTS, SLOT_ROWS, flat, HEAD), jnp.bfloat16),
            pltpu.VMEM((SLOTS, SLOT_ROWS, flat, HEAD), jnp.bfloat16),
            pltpu.VMEM((SLOT_ROWS * PAD_HEADS, HEAD), jnp.float32),
            pltpu.VMEM((2 * SLOT_ROWS * PAD_HEADS, HEAD), jnp.float32),
            pltpu.SemaphoreType.DMA((4, SLOTS)),
        ],
        compiler_params=pltpu.CompilerParams(vmem_limit_bytes=40 << 20),
        name="attend",
    )(lens, q, k_new, v_new, kc, vc)
    return ko.reshape(k_cache.shape), vo.reshape(v_cache.shape), out


def rotate(cols, cos_tab, sin_tab):
    rows, width = cols.shape
    heads = cols.reshape(rows, width // HEAD, HEAD)
    lower, upper = heads[..., :HEAD // 2], heads[..., HEAD // 2:]
    out = jnp.concatenate([lower * cos_tab - upper * sin_tab, upper * cos_tab + lower * sin_tab], axis=-1)
    return out.astype(jnp.bfloat16).astype(jnp.float32).reshape(rows, width)


def solution(mesh):
    mx_size = mesh.shape["mx"]
    act_spec = P(None, "mx")
    cache_spec = P("mx", None, "my", None)
    in_specs = (act_spec, P("mx"), P("mx"), P("mx"), P("mx", "my"), P("my"), P("mx", "my"), P("my"), P("mx", "my"), P("my"), P("my", "mx"), P("mx", "my"), P("mx", "my"), P("my", "mx"), cache_spec, cache_spec)
    out_specs = (act_spec, cache_spec, cache_spec)

    def local_layer(x_in, seq_lens, gain_attn, gain_mlp, w_q, b_q, w_k, b_k, w_v, b_v, w_o, w_gate, w_up, w_down, k_cache, v_cache):
        hidden = x_in.shape[1] * mx_size
        x_f32 = x_in.astype(jnp.float32)
        attn_sq = lax.psum(jnp.sum(x_f32 * x_f32, axis=1, keepdims=True), "mx")
        normed = (x_f32 * lax.rsqrt(attn_sq / hidden + NORM_EPS) * gain_attn.astype(jnp.float32)).astype(jnp.bfloat16)
        q_cols = w_q.shape[1]
        kv_cols = w_k.shape[1]
        partials = jnp.concatenate([
            jnp.dot(normed, w_q, preferred_element_type=jnp.float32).astype(jnp.bfloat16),
            jnp.dot(normed, w_k, preferred_element_type=jnp.float32).astype(jnp.bfloat16),
            jnp.dot(normed, w_v, preferred_element_type=jnp.float32).astype(jnp.bfloat16),
        ], axis=1)
        projected = lax.psum_scatter(partials, "mx", scatter_dimension=0, tiled=True).astype(jnp.float32)
        q_vals = projected[:, :q_cols] + b_q.astype(jnp.float32)
        k_vals = projected[:, q_cols:q_cols + kv_cols] + b_k.astype(jnp.float32)
        v_vals = projected[:, q_cols + kv_cols:] + b_v.astype(jnp.float32)
        half_dim = HEAD // 2
        inv_freq = ROPE_THETA ** (-2.0 * jnp.arange(half_dim, dtype=jnp.float32) / HEAD)
        angles = seq_lens.astype(jnp.float32)[:, None, None] * inv_freq
        cos_tab, sin_tab = jnp.cos(angles), jnp.sin(angles)
        q_rot = rotate(q_vals, cos_tab, sin_tab)
        k_rot = rotate(k_vals, cos_tab, sin_tab)
        v_new = v_vals.astype(jnp.bfloat16).astype(jnp.float32)
        k_cache_out, v_cache_out, attn_rows = attend(seq_lens, q_rot, k_rot, v_new, k_cache, v_cache)
        attn_all = lax.all_gather(attn_rows, "mx", axis=0, tiled=True)
        attn_proj = lax.psum(jnp.dot(attn_all, w_o, preferred_element_type=jnp.float32).astype(jnp.bfloat16), "my")
        x_mid = (x_f32 + attn_proj.astype(jnp.float32)).astype(jnp.bfloat16)
        mid_f32 = x_mid.astype(jnp.float32)
        mlp_sq = lax.psum(jnp.sum(mid_f32 * mid_f32, axis=1, keepdims=True), "mx")
        normed_mlp = (mid_f32 * lax.rsqrt(mlp_sq / hidden + NORM_EPS) * gain_mlp.astype(jnp.float32)).astype(jnp.bfloat16)
        ff_cols = w_gate.shape[1]
        gate_up = lax.psum(jnp.concatenate([
            jnp.dot(normed_mlp, w_gate, preferred_element_type=jnp.float32).astype(jnp.bfloat16),
            jnp.dot(normed_mlp, w_up, preferred_element_type=jnp.float32).astype(jnp.bfloat16),
        ], axis=1), "mx").astype(jnp.float32)
        hidden_act = (jax.nn.silu(gate_up[:, :ff_cols]) * gate_up[:, ff_cols:]).astype(jnp.bfloat16)
        down_proj = lax.psum(jnp.dot(hidden_act, w_down, preferred_element_type=jnp.float32).astype(jnp.bfloat16), "my")
        x_out = (mid_f32 + down_proj.astype(jnp.float32)).astype(jnp.bfloat16)
        return x_out, k_cache_out, v_cache_out

    return jax.shard_map(local_layer, mesh=mesh, in_specs=in_specs, out_specs=out_specs, check_vma=False)
```

time: 351 us -> 280 us (0.80)
  other arithmetic: 95.2 us -> 22.9 us
  Pallas kernels: 0 us -> 34.2 us
  matrix products: 78.6 us -> 49.2 us
  local copies, waits for them, and re-layouts: 12 us -> 6.9 us
    select_n x1 -> x0, other arithmetic: 68.6 us -> none  [local_layer(): v_cache_out = jnp.where(at_slot, v_new[:, None], v_cache)]
    pallas_call x0 -> x1, Pallas kernels: none -> 34.2 us  [attend(): pl.pallas_call(attend_kernel, out_shape=(jax.ShapeDtypeStruct(kc.shape, k...]
    dot_general x2 -> x0, matrix products: 29 us -> none  [the longest x1 16.7 us: attend_local(): jnp.einsum('bkgd,bskd->bkgs', q_grouped, k_cache_out, preferred_element_t...]
    concatenate x2 -> x0, local copies, waits for them, and re-layouts: 4.12 us -> none  [apply_rotary(): jnp.concatenate([lower_half * cos_tab - upper_half * sin_tab, upper_half...]
where the time goes in v1:
time: 280 us
  waiting for transfers between devices  144 us (51%)
  matrix products  49.2 us (18%)
  Pallas kernels  34.2 us (12%)
  other arithmetic  22.9 us (8%)
  between operations  14.1 us (5%)
  blocking collectives  8.59 us (3%)
  local copies, waits for them, and re-layouts  6.9 us (2%)
    psum x1, waiting for transfers between devices, local_layer(): lax.psum(jnp.dot(attn_all, w_o, preferred_element_type=jnp.float32).astyp...  57.1 us
    psum x1, waiting for transfers between devices, local_layer(): lax.psum(jnp.dot(hidden_act, w_down, preferred_element_type=jnp.float32)....  57 us
    pallas_call x1, Pallas kernels, attend(): pl.pallas_call(attend_kernel, out_shape=(jax.ShapeDtypeStruct(kc.shape, k...  34.2 us
    psum x1, waiting for transfers between devices, local_layer(): lax.psum(jnp.concatenate([jnp.dot(normed_mlp, w_gate, preferred_element_t...  23.1 us
    dot_general x1, matrix products, local_layer(): jnp.dot(hidden_act, w_down, preferred_element_type=jnp.float32)  13.6 us
    dot_general x1, matrix products, local_layer(): jnp.dot(normed_mlp, w_up, preferred_element_type=jnp.float32)  11.9 us
    dot_general x1, matrix products, local_layer(): jnp.dot(normed_mlp, w_gate, preferred_element_type=jnp.float32)  11.2 us
    dot_general x1, matrix products, local_layer(): jnp.dot(attn_all, w_o, preferred_element_type=jnp.float32)  6.72 us
  transfers between devices with their start and end apart: 4, of which 4 were waited for; matrix products, arithmetic and copies ran while one was open for 1% of the time, Pallas kernels for 0%

profile of v1, /device:TPU:0, one launch (start us, length us, event | category | flops | bytes accessed | tf_op | source)
XLA Modules:
  0.0 279.7 jit_solution(989699943362566328)
XLA Ops:
  7.2 2.1 fusion.1
  9.3 3.1 %psum.35 = f32[384,1]{0,1:T(1,128)S(1)} all-reduce(f32[384,1]{0,1:T(1,128)S(1)} %broadcast_in_dim.4), channel_id=1, replica_groups=mesh['my'=4,'mx'=2] {'mx'}, use_global_device_ids=true, to_apply=%region_1.0 | all-reduce | flops 384 | bytes 3072 | tf_op jit(solution)/shard_map/psum | solution.py:154
  13.3 2.3 convolution_convert_fusion.6
  16.4 2.1 copy-done.9
  18.5 2.8 convolution_convert_fusion.4
  24.4 6.4 %reduce-scatter.2.cloned.1.call-done = bf16[192,1792]{1,0:T(8,128)(2,1)} async-done(((bf16[384,1792]{1,0:T(8,128)(2,1)}), bf16[192,1792]{1,0:T(8,128)(2,1)}) %reduce-scatter.2.cloned.1.call-update) | async-done | bytes 688144 | tf_op jit(solution)/shard_map/reduce_scatter | solution.py:163
  32.3 1.3 subtract_convert_fusion.1
  33.8 1.5 copy.23
  35.3 1.5 subtract_convert_fusion
  38.1 1.7 copy.26.q_ref
  39.8 34.2 %attend.1 = (bf16[192,512,128]{2,1,0:T(8,128)(2,1)}, bf16[192,512,128]{2,1,0:T(8,128)(2,1)}, bf16[192,1280]{1,0:T(8,128)(2,1)S(1)}) custom-call(s32[192]{0:T(256)S(1)} %copy-done.2, f32[192,1280]{1,0:T(8,128)S(1)} %copy.26.q_ref, f32[192,256]{1,0:T(8,128)S(1)} %bitcast.20, f32[192,256]{1,0:T(8,128)S(1)} %get-tuple-element.13.vn_ref, ...), custom_call_target="tpu_custom_call" | custom-call | tf_op jit(solution)/shard_map/attend/pallas_call | solution.py:118
  73.9 2.8 %all_gather.3 = bf16[384,1280]{1,0:T(8,128)(2,1)S(1)} all-gather(bf16[192,1280]{1,0:T(8,128)(2,1)S(1)} %get-tuple-element.6), channel_id=1, replica_groups=mesh['my'=4,'mx'=2] {'mx'}, dimensions={0}, use_global_device_ids=true | all-gather | bytes 1474560 | tf_op jit(solution)/shard_map/all_gather | solution.py:175
  76.8 6.7 %convolution_convert_fusion.2 = bf16[384,2560]{1,0:T(8,128)(2,1)} fusion(bf16[384,1280]{1,0:T(8,128)(2,1)S(1)} %all_gather.3, bf16[1280,2560]{1,0:T(8,128)(2,1)} %param.26), kind=kOutput, calls=%fused_computation.11 | convolution fusion | flops 2517565440 | bytes 9502720 | tf_op jit(solution)/shard_map/dot_general | solution.py:176
  83.6 57.1 %all-reduce.4.cloned.1.call-done = bf16[384,2560]{1,0:T(8,128)(2,1)} async-done(((bf16[384,2560]{1,0:T(8,128)(2,1)}), bf16[384,2560]{1,0:T(8,128)(2,1)}) %all-reduce.4.cloned.1.call-update) | async-done | bytes 1966096 | tf_op jit(solution)/shard_map/psum | solution.py:176
  140.7 3.7 %fusion.5 = (f32[384]{0:T(512)S(1)}, bf16[384,2560]{1,0:T(8,128)(2,1)}) fusion(bf16[384,2560]{1,0:T(8,128)(2,1)} %all-reduce.4.cloned.1.call-done, bf16[384,2560]{1,0:T(8,128)(2,1)S(1)} %copy-done.3), kind=kLoop, calls=%fused_computation.17 | loop fusion | flops 6880896 | bytes 5899776 | tf_op jit(solution)/shard_map/reduce_sum | solution.py:179
  144.4 2.6 psum.37
  147.1 11.9 %convolution_convert_fusion = bf16[384,3456]{1,0:T(8,128)(2,1)S(1)} fusion(bf16[2560,3456]{1,0:T(8,128)(2,1)} %param.28, bf16[384,2560]{1,0:T(8,128)(2,1)} %get-tuple-element.10, f32[2560]{0:T(1024)S(1)} %convert_element_type.119, f32[384]{0:T(512)S(1)} %rsqrt_reduce_fusion), kind=kOutput, calls=%fused_computation.6 | convolution fusion | flops 6800031744 | bytes 22326784 | tf_op jit(solution)/shard_map/dot_general | solution.py:184
  159.0 11.2 %convolution_convert_fusion.1 = bf16[384,3456]{1,0:T(8,128)(2,1)S(1)} fusion(bf16[2560,3456]{1,0:T(8,128)(2,1)} %param.27, bf16[384,2560]{1,0:T(8,128)(2,1)S(1)} %copy-done.4, f32[2560]{0:T(1024)S(1)} %convert_element_type.119, f32[384]{0:T(512)S(1)} %rsqrt_reduce_fusion), kind=kOutput, calls=%fused_computation.7 | convolution fusion | flops 6800031744 | bytes 22326784 | tf_op jit(solution)/shard_map/dot_general | solution.py:183
  170.2 2.7 pad_maximum_fusion
  173.0 23.1 %all-reduce.6.cloned.1.call-done = bf16[384,6912]{1,0:T(8,128)(2,1)} async-done(((bf16[384,6912]{1,0:T(8,128)(2,1)}), bf16[384,6912]{1,0:T(8,128)(2,1)}) %all-reduce.6.cloned.1.call-update) | async-done | bytes 5308432 | tf_op jit(solution)/shard_map/psum | solution.py:182
  196.1 3.2 %convert_element_type.123 = f32[384,6912]{1,0:T(8,128)S(1)} convert(bf16[384,6912]{1,0:T(8,128)(2,1)} %all-reduce.6.cloned.1.call-done) | non-fusion elementwise | flops 2654208 | bytes 15925248 | tf_op jit(solution)/shard_map/convert_element_type | solution.py:185
  199.3 13.6 %convolution_convert_fusion.3 = bf16[384,2560]{1,0:T(8,128)(2,1)} fusion(bf16[3456,2560]{1,0:T(8,128)(2,1)} %param.29, f32[384,6912]{1,0:T(8,128)S(1)} %convert_element_type.123), kind=kOutput, calls=%fused_computation.12 | convolution fusion | flops 6803718144 | bytes 30277632 | tf_op jit(solution)/shard_map/dot_general | solution.py:187
  212.9 57.0 %all-reduce.8.cloned.1.call-done = bf16[384,2560]{1,0:T(8,128)(2,1)} async-done(((bf16[384,2560]{1,0:T(8,128)(2,1)}), bf16[384,2560]{1,0:T(8,128)(2,1)}) %all-reduce.8.cloned.1.call-update) | async-done | bytes 1966096 | tf_op jit(solution)/shard_map/psum | solution.py:187
  269.9 3.3 %fusion.8 = bf16[384,2560]{1,0:T(8,128)(2,1)} fusion(bf16[384,2560]{1,0:T(8,128)(2,1)S(1)} %copy-done.4, bf16[384,2560]{1,0:T(8,128)(2,1)} %all-reduce.8.cloned.1.call-done), kind=kLoop, calls=%fused_computation.20 | loop fusion | flops 3932160 | bytes 5898240 | tf_op jit(solution)/shard_map/convert_element_type | solution.py:188
  (57 shorter events, 7.9 us)
Async XLA Ops:
  7.2 6.1 %copy-start = (bf16[2560,256]{1,0:T(8,128)(2,1)S(1)}, bf16[2560,256]{1,0:T(8,128)(2,1)}, u32[]{:S(2)}) copy-start(bf16[2560,256]{1,0:T(8,128)(2,1)} %param.22) | copy-start | bytes 3932164
  7.2 23.6 %reduce-scatter.2.cloned.1.call-start = ((), (), s32[]{:S(2)}) async-start(), calls=%async_computation.1 | async-start | bytes 2064384 | tf_op jit(solution)/shard_map/reduce_scatter | solution.py:163
  9.3 6.2 %copy-start.3 = (bf16[384,2560]{1,0:T(8,128)(2,1)S(1)}, bf16[384,2560]{1,0:T(8,128)(2,1)}, u32[]{:S(2)}) copy-start(bf16[384,2560]{1,0:T(8,128)(2,1)} %param.16) | copy-start | bytes 5898244
  12.5 3.1 %copy-start.10 = (bf16[2560,256]{1,0:T(8,128)(2,1)S(1)}, bf16[2560,256]{1,0:T(8,128)(2,1)}, u32[]{:S(2)}) copy-start(bf16[2560,256]{1,0:T(8,128)(2,1)} %param.24) | copy-start | bytes 3932164
  15.6 2.9 %copy-start.9 = (bf16[2560,1280]{1,0:T(8,128)(2,1)S(1)}, bf16[2560,1280]{1,0:T(8,128)(2,1)}, u32[]{:S(2)}) copy-start(bf16[2560,1280]{1,0:T(8,128)(2,1)} %param.20) | copy-start | bytes 19660804
  21.2 1.3 copy-start.11
  21.3 1.3 copy-start.12
  21.3 1.3 copy-start.2
  21.3 1.3 copy-start.8
  22.5 118.2 %all-reduce.4.cloned.1.call-start = ((), (), s32[]{:S(2)}) async-start(), calls=%async_computation.2 | async-start | bytes 3932160 | tf_op jit(solution)/shard_map/psum | solution.py:176
  22.9 7.9 %copy-start.5 = (f32[192,64]{0,1:T(8,128)}, f32[192,64]{0,1:T(8,128)S(1)}, u32[]{:S(2)}) copy-start(f32[192,64]{0,1:T(8,128)S(1)} %get-tuple-element.17) | copy-start | bytes 147460
  23.0 7.9 %copy-start.6 = (f32[192,64]{0,1:T(8,128)}, f32[192,64]{0,1:T(8,128)S(1)}, u32[]{:S(2)}) copy-start(f32[192,64]{0,1:T(8,128)S(1)} %get-tuple-element.18) | copy-start | bytes 147460
  76.8 6.8 %copy-start.7 = (bf16[2560]{0:T(1024)(128)(2,1)S(1)}, bf16[2560]{0:T(1024)(128)(2,1)}, u32[]{:S(2)}) copy-start(bf16[2560]{0:T(1024)(128)(2,1)} %param.19) | copy-start | bytes 15364
  83.5 112.6 %all-reduce.6.cloned.1.call-start = ((), (), s32[]{:S(2)}) async-start(), calls=%async_computation.3 | async-start | bytes 10616832 | tf_op jit(solution)/shard_map/psum | solution.py:182
  147.1 11.9 %copy-start.4 = (bf16[384,2560]{1,0:T(8,128)(2,1)S(1)}, bf16[384,2560]{1,0:T(8,128)(2,1)}, u32[]{:S(2)}) copy-start(bf16[384,2560]{1,0:T(8,128)(2,1)} %get-tuple-element.10) | copy-start | bytes 5898244
  172.9 97.0 %all-reduce.8.cloned.1.call-start = ((), (), s32[]{:S(2)}) async-start(), calls=%async_computation.4 | async-start | bytes 3932160 | tf_op jit(solution)/shard_map/psum | solution.py:187
  212.9 60.3 %copy-start.1 = (bf16[2560,256]{1,0:T(8,128)(2,1)S(1)}, bf16[2560,256]{1,0:T(8,128)(2,1)}, u32[]{:S(2)}) copy-start(bf16[2560,256]{1,0:T(8,128)(2,1)} %param.22) | copy-start | bytes 3932164
Sparse Core Ops, SparseCore 0:
  22.6 8.1 reduce-scatter.1
  83.7 57.0 all-reduce.3
  173.0 23.0 all-reduce.5
  213.0 56.8 all-reduce.7

commit v2 on v1

--- a/solution.py
+++ b/solution.py
@@ -12,6 +12,13 @@
 SLOTS = 8
 AHEAD = 6
 PAD_HEADS = 16
+CHUNKS = 1
+RING = 6
+PIECE = 640
+TILE = 256
+MROWS = 192
+ROWS_STEP = 16
+MESH = pl.DeviceIdType.MESH
 
 
 def attend_kernel(lens, q_ref, kn_ref, vn_ref, kc, vc, ko, vo, out_ref, kbuf, vbuf, qs, os, sems):
@@ -133,6 +140,322 @@
     return ko.reshape(k_cache.shape), vo.reshape(v_cache.shape), out
 
 
+def tail_kernel(attn_ref, x_hbm, gain_ref, wo_hbm, wg_hbm, wu_hbm, wd_hbm, out_ref,
+                attn_all, xown, wo_v, wd_v, ring, sb, rb, keep, mall, hbuf, gsend, grecv, act, ssq, ssr,
+                wo_sem, wd_sem, ring_sem, x_sem, ici_ss, ici_rs, gu_ss, gu_rs, act_ss, act_rs, st_ss, st_rs, at_ss, at_rs):
+    my, mx = lax.axis_index("my"), lax.axis_index("mx")
+    row_count, hidden = out_ref.shape
+    half_rows = row_count // 2
+    sub = half_rows // CHUNKS
+    ff = wg_hbm.shape[1]
+    steps = (ff // 128 + 1) // 2 * 128 // TILE
+    own_w = steps * TILE
+    shift = ff - own_w
+    per_chunk = 2 * steps
+    total_steps = CHUNKS * per_chunk
+
+    def chunk_of(r):
+        return lax.rem(my // 2 + r // 2, 2) * 2 + lax.rem(lax.rem(my, 2) + r % 2, 2)
+
+    def device(r):
+        return (chunk_of(r), mx)
+
+    partner = (my, 1 - mx)
+    first = lambda s: 1 if s == 0 else 2
+    second = lambda s: 2 if s == 0 else 1
+
+    def cols(r):
+        return pl.ds(pl.multiple_of(chunk_of(r) * PIECE, 128), PIECE)
+
+    barrier = pltpu.get_barrier_semaphore()
+    for peer in (device(1), device(2), partner):
+        pl.semaphore_signal(barrier, inc=1, device_id=peer, device_id_type=MESH)
+
+    order = (3, 1, 2, 0)
+    wo_copies = {r: pltpu.make_async_copy(wo_hbm.at[:, cols(r)], wo_v.at[r], wo_sem.at[r]) for r in order}
+    wd_copies = {r: pltpu.make_async_copy(wd_hbm.at[:, cols(r)], wd_v.at[r], wd_sem.at[r]) for r in order}
+    x_copy = pltpu.make_async_copy(x_hbm.at[:, cols(0)], xown, x_sem)
+    for r in order:
+        wo_copies[r].start()
+    x_copy.start()
+
+    def ring_copies(g):
+        slot = lax.rem(g, RING)
+        at = lax.rem(g, per_chunk)
+        mine = at // steps
+        side = mine * mx + (1 - mine) * (1 - mx)
+        col = pl.multiple_of(side * shift + lax.rem(at, steps) * TILE, 128)
+        return (pltpu.make_async_copy(wg_hbm.at[:, pl.ds(col, TILE)], ring.at[slot, :, pl.ds(0, TILE)], ring_sem.at[slot, 0]),
+                pltpu.make_async_copy(wu_hbm.at[:, pl.ds(col, TILE)], ring.at[slot, :, pl.ds(TILE, TILE)], ring_sem.at[slot, 1]))
+
+    def remote(src, dst, ss, rs, peer):
+        return pltpu.make_async_remote_copy(src_ref=src, dst_ref=dst, send_sem=ss, recv_sem=rs, device_id=peer, device_id_type=MESH)
+
+    def hop(c, s, msg, src, dst, r):
+        return remote(src, dst, ici_ss.at[c, s, msg], ici_rs.at[c, s, msg], device(r))
+
+    pl.semaphore_wait(barrier, 3)
+    attn_msg = remote(attn_ref, attn_all.at[mx], at_ss, at_rs, partner)
+    attn_msg.start()
+
+    def for_rows(count, body):
+        @pl.loop(0, count // ROWS_STEP)
+        def _(i):
+            body(pl.multiple_of(i * ROWS_STEP, ROWS_STEP))
+
+    def copy_attn(at):
+        attn_all[mx, pl.ds(at, ROWS_STEP), :] = attn_ref[pl.ds(at, ROWS_STEP), :]
+    for_rows(half_rows, copy_attn)
+
+    def rs_msg(c, s, base, k):
+        return hop(c, s, base + k, sb.at[c, s, k], rb.at[c, s, k], second(s) if k == 2 else first(s))
+
+    blocks = 2 * sub // MROWS
+
+    def parts(block):
+        if CHUNKS == 1:
+            return ((block, 0, sub),)
+        return ((0, 0, sub), (1, sub, 2 * sub))
+
+    def product(c, r, lhs, weights, base, send):
+        for block in range(blocks):
+            acc = jnp.dot(lhs(block), weights[...], preferred_element_type=jnp.float32)
+            for s, lo, hi in parts(block):
+                piece = acc[lo:hi]
+                if r == 3 or r == first(s):
+                    which = 0 if r == 3 else 1
+                    sb[c, s, which] = piece.astype(jnp.bfloat16)
+                    if send:
+                        rs_msg(c, s, base, which).start()
+                else:
+                    keep[c, s, 0 if r == second(s) else 1] = piece
+
+    def rs_send(c, base):
+        for which in range(2):
+            for s in range(2):
+                rs_msg(c, s, base, which).start()
+
+    def rs_middle(c, base):
+        for s in range(2):
+            rs_msg(c, s, base, 0).wait_recv()
+
+            def add(at, s=s):
+                rows = pl.ds(at, ROWS_STEP)
+                sb[c, s, 2, rows, :] = (keep[c, s, 0, rows, :] + rb[c, s, 0, rows, :].astype(jnp.float32)).astype(jnp.bfloat16)
+            for_rows(sub, add)
+            rs_msg(c, s, base, 2).start()
+
+    def rs_sum(c, s, rows):
+        return keep[c, s, 1, rows, :] + rb[c, s, 1, rows, :].astype(jnp.float32) + rb[c, s, 2, rows, :].astype(jnp.float32)
+
+    def mid_at(c, s, r):
+        return mall.at[c, chunk_of(r), pl.ds(s * sub, sub), :]
+
+    def out_at(c, s, r):
+        return out_ref.at[pl.ds(s * half_rows + c * sub, sub), cols(r)]
+
+    def ag_msg(c, s, base, at, k):
+        src = at(c, s, second(s) if k == 2 else 0)
+        return hop(c, s, base + k, src, src, second(s) if k == 0 else first(s))
+
+    def finish_mid(c):
+        for s in range(2):
+            rs_msg(c, s, 0, 1).wait_recv()
+            rs_msg(c, s, 0, 2).wait_recv()
+
+            def add(at, s=s):
+                rows = pl.ds(at, ROWS_STEP)
+                total = rs_sum(c, s, rows) + xown[pl.ds(s * half_rows + c * sub + at, ROWS_STEP), :].astype(jnp.float32)
+                mall[c, my, pl.ds(s * sub + at, ROWS_STEP), :] = total.astype(jnp.bfloat16)
+            for_rows(sub, add)
+            ag_msg(c, s, 3, mid_at, 0).start()
+            ag_msg(c, s, 3, mid_at, 1).start()
+
+    def finish_out(c):
+        for s in range(2):
+            rs_msg(c, s, 6, 1).wait_recv()
+            rs_msg(c, s, 6, 2).wait_recv()
+
+            def add(at, s=s):
+                rows = pl.ds(at, ROWS_STEP)
+                total = rs_sum(c, s, rows) + mall[c, my, pl.ds(s * sub + at, ROWS_STEP), :].astype(jnp.float32)
+                out_ref[pl.ds(s * half_rows + c * sub + at, ROWS_STEP), cols(0)] = total.astype(jnp.bfloat16)
+            for_rows(sub, add)
+            ag_msg(c, s, 9, out_at, 0).start()
+            ag_msg(c, s, 9, out_at, 1).start()
+
+    def forward(c, base, at):
+        for s in range(2):
+            ag_msg(c, s, base, at, 0).wait_recv()
+            ag_msg(c, s, base, at, 2).start()
+
+    def arrive(c, base, at):
+        for s in range(2):
+            ag_msg(c, s, base, at, 1).wait_recv()
+            ag_msg(c, s, base, at, 2).wait_recv()
+
+    def sent(c, base, at=None):
+        for s in range(2):
+            for k in range(3):
+                (rs_msg(c, s, base, k) if at is None else ag_msg(c, s, base, at, k)).wait_send()
+
+    def normalise(c):
+        def squares(at):
+            rows = pl.ds(at, ROWS_STEP)
+            total = jnp.zeros((ROWS_STEP, 128), jnp.float32)
+            for j in range(4):
+                for k in range(0, PIECE, 128):
+                    m = mall[c, j, rows, k:k + 128].astype(jnp.float32)
+                    total = total + m * m
+            ssq[c, rows, :] = total
+        for_rows(2 * sub, squares)
+        msg = remote(ssq.at[c], ssr.at[c], st_ss.at[c], st_rs.at[c], partner)
+        msg.start()
+        msg.wait()
+
+        def scale(at):
+            rows = pl.ds(at, ROWS_STEP)
+            total = jnp.sum(ssq[c, rows, :] + ssr[c, rows, :], axis=1, keepdims=True)
+            inv = lax.rsqrt(total / (2 * hidden) + NORM_EPS)
+            for j in range(4):
+                at_col = slice(j * PIECE, (j + 1) * PIECE)
+                hbuf[rows, at_col] = (mall[c, j, rows, :].astype(jnp.float32) * inv * gain_ref[:, at_col]).astype(jnp.bfloat16)
+        for_rows(2 * sub, scale)
+
+    def gu_msg(c, t):
+        return remote(gsend.at[t], grecv.at[t], gu_ss.at[c, t], gu_rs.at[c, t], partner)
+
+    def tiles(c, mine, lo, hi):
+        @pl.loop(lo, hi)
+        def _(t):
+            g = c * per_chunk + mine * steps + t
+            slot = lax.rem(g, RING)
+            for copy in ring_copies(g):
+                copy.wait()
+            if mine:
+                gu_msg(c, t).wait_recv()
+            for block in range(blocks):
+                rows = slice(block * MROWS, (block + 1) * MROWS)
+                acc = jnp.dot(hbuf[rows, :], ring[slot], preferred_element_type=jnp.float32)
+                if mine:
+                    both = acc + grecv[t, rows, :].astype(jnp.float32)
+                    gate, up = both[:, :TILE], both[:, TILE:]
+                    act[rows, pl.ds(pl.multiple_of(mx * shift + t * TILE, 128), TILE)] = (gate * jax.nn.sigmoid(gate) * up).astype(jnp.bfloat16)
+                else:
+                    gsend[t, rows, :] = acc.astype(jnp.bfloat16)
+            if not mine:
+                gu_msg(c, t).start()
+
+            @pl.when(g + RING < total_steps)
+            def _():
+                for copy in ring_copies(g + RING):
+                    copy.start()
+
+    cut = 3 * TILE
+
+    def act_msg(c, k):
+        width = cut if k == 0 else shift - cut
+        where = pl.ds(pl.multiple_of(mx * own_w + (0 if k == 0 else cut), 128), width)
+        return remote(act.at[:, where], act.at[:, where], act_ss.at[c, k], act_rs.at[c, k], partner)
+
+    def gates_sent(c):
+        for t in range(steps):
+            gu_msg(c, t).wait_send()
+
+    def attn_lhs(c):
+        def get(block):
+            if CHUNKS == 1:
+                return attn_all[block]
+            rows = slice(c * sub, (c + 1) * sub)
+            return jnp.concatenate([attn_all[0, rows, :], attn_all[1, rows, :]], axis=0)
+        return get
+
+    def act_lhs(block):
+        return act[block * MROWS:(block + 1) * MROWS, :]
+
+    attn_msg.wait_recv()
+    for r in order:
+        wo_copies[r].wait()
+        if r == 3:
+            for g in range(RING):
+                for copy in ring_copies(g):
+                    copy.start()
+        product(0, r, attn_lhs(0), wo_v.at[r], 0, True)
+    x_copy.wait()
+    for r in order:
+        wd_copies[r].start()
+    rs_middle(0, 0)
+    finish_mid(0)
+    forward(0, 3, mid_at)
+    arrive(0, 3, mid_at)
+    normalise(0)
+    tiles(0, 0, 0, steps)
+    tiles(0, 1, 0, 4)
+    act_msg(0, 0).start()
+    tiles(0, 1, 4, steps)
+    act_msg(0, 1).start()
+    sent(0, 0)
+    for k in range(2):
+        act_msg(0, k).wait_recv()
+    for r in order:
+        wd_copies[r].wait()
+        product(0, r, act_lhs, wd_v.at[r], 6, True)
+    rs_middle(0, 6)
+    finish_out(0)
+    forward(0, 9, out_at)
+    arrive(0, 9, out_at)
+    gates_sent(0)
+    for k in range(2):
+        act_msg(0, k).wait_send()
+    sent(0, 3, mid_at)
+    sent(0, 6)
+    sent(0, 9, out_at)
+    attn_msg.wait_send()
+
+
+def tail(attn, x_in, gain, w_o, w_gate, w_up, w_down):
+    rows, hidden = x_in.shape
+    q_width = w_o.shape[0]
+    ff = w_gate.shape[1]
+    sub = rows // 2 // CHUNKS
+    steps = (ff // 128 + 1) // 2 * 128 // TILE
+    whole = pl.BlockSpec(memory_space=pltpu.VMEM)
+    hbm = pl.BlockSpec(memory_space=pltpu.HBM)
+    bf16, f32 = jnp.bfloat16, jnp.float32
+    dma = pltpu.SemaphoreType.DMA
+    return pl.pallas_call(
+        tail_kernel,
+        out_shape=jax.ShapeDtypeStruct((rows, hidden), bf16),
+        in_specs=[whole, hbm, whole, hbm, hbm, hbm, hbm],
+        out_specs=whole,
+        scratch_shapes=[
+            pltpu.VMEM((2, rows // 2, q_width), bf16),
+            pltpu.VMEM((rows, PIECE), bf16),
+            pltpu.VMEM((4, q_width, PIECE), bf16),
+            pltpu.VMEM((4, ff, PIECE), bf16),
+            pltpu.VMEM((RING, hidden, 2 * TILE), bf16),
+            pltpu.VMEM((CHUNKS, 2, 3, sub, PIECE), bf16),
+            pltpu.VMEM((CHUNKS, 2, 3, sub, PIECE), bf16),
+            pltpu.VMEM((CHUNKS, 2, 2, sub, PIECE), f32),
+            pltpu.VMEM((CHUNKS, 4, 2 * sub, PIECE), bf16),
+            pltpu.VMEM((2 * sub, hidden), bf16),
+            pltpu.VMEM((steps, 2 * sub, 2 * TILE), bf16),
+            pltpu.VMEM((steps, 2 * sub, 2 * TILE), bf16),
+            pltpu.VMEM((2 * sub, ff), bf16),
+            pltpu.VMEM((CHUNKS, 2 * sub, 128), f32),
+            pltpu.VMEM((CHUNKS, 2 * sub, 128), f32),
+            dma((4,)), dma((4,)), dma((RING, 2)), dma(()),
+            dma((CHUNKS, 2, 12)), dma((CHUNKS, 2, 12)),
+            dma((CHUNKS, steps)), dma((CHUNKS, steps)),
+            dma((CHUNKS, 2)), dma((CHUNKS, 2)),
+            dma((CHUNKS,)), dma((CHUNKS,)),
+            dma(()), dma(()),
+        ],
+        compiler_params=pltpu.CompilerParams(collective_id=1, has_side_effects=True, vmem_limit_bytes=67043328),
+        name="tail",
+    )(attn, x_in, gain, w_o, w_gate, w_up, w_down)
+
+
 def rotate(cols, cos_tab, sin_tab):
     rows, width = cols.shape
     heads = cols.reshape(rows, width // HEAD, HEAD)
@@ -172,20 +495,7 @@
         k_rot = rotate(k_vals, cos_tab, sin_tab)
         v_new = v_vals.astype(jnp.bfloat16).astype(jnp.float32)
         k_cache_out, v_cache_out, attn_rows = attend(seq_lens, q_rot, k_rot, v_new, k_cache, v_cache)
-        attn_all = lax.all_gather(attn_rows, "mx", axis=0, tiled=True)
-        attn_proj = lax.psum(jnp.dot(attn_all, w_o, preferred_element_type=jnp.float32).astype(jnp.bfloat16), "my")
-        x_mid = (x_f32 + attn_proj.astype(jnp.float32)).astype(jnp.bfloat16)
-        mid_f32 = x_mid.astype(jnp.float32)
-        mlp_sq = lax.psum(jnp.sum(mid_f32 * mid_f32, axis=1, keepdims=True), "mx")
-        normed_mlp = (mid_f32 * lax.rsqrt(mlp_sq / hidden + NORM_EPS) * gain_mlp.astype(jnp.float32)).astype(jnp.bfloat16)
-        ff_cols = w_gate.shape[1]
-        gate_up = lax.psum(jnp.concatenate([
-            jnp.dot(normed_mlp, w_gate, preferred_element_type=jnp.float32).astype(jnp.bfloat16),
-            jnp.dot(normed_mlp, w_up, preferred_element_type=jnp.float32).astype(jnp.bfloat16),
-        ], axis=1), "mx").astype(jnp.float32)
-        hidden_act = (jax.nn.silu(gate_up[:, :ff_cols]) * gate_up[:, ff_cols:]).astype(jnp.bfloat16)
-        down_proj = lax.psum(jnp.dot(hidden_act, w_down, preferred_element_type=jnp.float32).astype(jnp.bfloat16), "my")
-        x_out = (mid_f32 + down_proj.astype(jnp.float32)).astype(jnp.bfloat16)
+        x_out = tail(attn_rows, x_in, gain_mlp.astype(jnp.float32)[None, :], w_o, w_gate, w_up, w_down)
         return x_out, k_cache_out, v_cache_out
 
     return jax.shard_map(local_layer, mesh=mesh, in_specs=in_specs, out_specs=out_specs, check_vma=False)

time: 280 us -> 185 us (0.66)
  waiting for transfers between devices: 144 us -> 7.16 us
  Pallas kernels: 34.2 us -> 141 us
  matrix products: 49.2 us -> 5.64 us
  other arithmetic: 22.9 us -> 6.1 us
  blocking collectives: 8.59 us -> 2.99 us
    psum x3 -> x0, waiting for transfers between devices: 137 us -> none  [the longest x1 57.1 us: local_layer(): lax.psum(jnp.dot(attn_all, w_o, preferred_element_type=jnp.float32).astyp...]
    pallas_call x0 -> x1, Pallas kernels: none -> 106 us  [tail(): pl.pallas_call(tail_kernel, out_shape=jax.ShapeDtypeStruct((rows, hidden)...]
    dot_general x4 -> x0, matrix products: 43.4 us -> none  [the longest x1 13.6 us: local_layer(): jnp.dot(hidden_act, w_down, preferred_element_type=jnp.float32)]
    convert_element_type x3 -> x0, other arithmetic: 6.46 us -> none  [the longest x1 3.26 us: local_layer(): x_out = (mid_f32 + down_proj.astype(jnp.float32)).astype(jnp.bfloat16)]
    unnamed x27 -> x22, local copies, waits for them, and re-layouts: 2.15 us -> 5.88 us
    reduce_sum x1 -> x0, other arithmetic: 3.7 us -> none  [local_layer(): mlp_sq = lax.psum(jnp.sum(mid_f32 * mid_f32, axis=1, keepdims=True), 'mx')]
    all_gather x1 -> x0, blocking collectives: 2.84 us -> none  [local_layer(): attn_all = lax.all_gather(attn_rows, 'mx', axis=0, tiled=True)]
  transfers between devices with their start and end apart: 4 -> 1, of which waited for: 4 -> 1; matrix products, arithmetic and copies ran while one was open for 1% -> 1% of each run, Pallas kernels for 0% -> 0%
where the time goes in v2:
time: 185 us; the launch traced here: 184 us
  Pallas kernels  141 us (76%)
  between operations  14.4 us (8%)
  local copies, waits for them, and re-layouts  7.56 us (4%)
  waiting for transfers between devices  7.16 us (4%)
  other arithmetic  6.1 us (3%)
  matrix products  5.64 us (3%)
  blocking collectives  2.99 us (2%)
    pallas_call x1, Pallas kernels, tail(): pl.pallas_call(tail_kernel, out_shape=jax.ShapeDtypeStruct((rows, hidden)...  106 us
    pallas_call x1, Pallas kernels, attend(): pl.pallas_call(attend_kernel, out_shape=(jax.ShapeDtypeStruct(kc.shape, k...  34.7 us
    reduce_scatter x1, waiting for transfers between devices, local_layer(): lax.psum_scatter(partials, 'mx', scatter_dimension=0, tiled=True)  7.15 us
    unnamed x22, local copies, waits for them, and re-layouts  5.88 us
  transfers between devices with their start and end apart: 1, of which 1 were waited for; matrix products, arithmetic and copies ran while one was open for 1% of the time, Pallas kernels for 0%

profile of v2, /device:TPU:0, one launch (start us, length us, event | category | flops | bytes accessed | tf_op | source)
XLA Modules:
  0.0 184.4 jit_solution(15320720916595044274)
XLA Ops:
  7.2 2.1 %fusion = f32[384]{0:T(512)S(1)} fusion(bf16[384,2560]{1,0:T(8,128)(2,1)} %x_hbm.1), kind=kLoop, calls=%fused_computation.2 | loop fusion | flops 2948736 | bytes 1967616 | tf_op jit(solution)/shard_map/reduce_sum | solution.py:477
  9.4 3.0 %psum.7 = f32[384,1]{0,1:T(1,128)S(1)} all-reduce(f32[384,1]{0,1:T(1,128)S(1)} %broadcast_in_dim.6), channel_id=1, replica_groups=mesh['my'=4,'mx'=2] {'mx'}, use_global_device_ids=true, to_apply=%region_1.0 | all-reduce | flops 384 | bytes 3072 | tf_op jit(solution)/shard_map/psum | solution.py:477
  12.4 2.2 %convolution_convert_fusion.2 = bf16[384,256]{1,0:T(8,128)(2,1)S(1)} fusion(bf16[2560,256]{1,0:T(8,128)(2,1)} %param.22, bf16[384,2560]{1,0:T(8,128)(2,1)S(1)} %copy-done.2, f32[2560]{0:T(1024)S(1)} %convert_element_type.61, f32[384]{0:T(512)S(1)} %rsqrt_reduce_fusion), kind=kOutput, calls=%fused_computation.8 | convolution fusion | flops 507346944 | bytes 3485184 | tf_op jit(solution)/shard_map/dot_general | solution.py:483
  14.6 0.7 convolution_convert_fusion.1
  15.4 2.1 %copy-done.6 = bf16[2560,1280]{1,0:T(8,128)(2,1)S(1)} copy-done((bf16[2560,1280]{1,0:T(8,128)(2,1)S(1)}, bf16[2560,1280]{1,0:T(8,128)(2,1)}, u32[]{:S(2)}) %copy-start.6) | copy-done | bytes 6553624
  17.5 2.7 %convolution_convert_fusion = bf16[384,1280]{1,0:T(8,128)(2,1)S(1)} fusion(bf16[2560,1280]{1,0:T(8,128)(2,1)S(1)} %copy-done.6, bf16[384,2560]{1,0:T(8,128)(2,1)S(1)} %copy-done.2, f32[2560]{0:T(1024)S(1)} %convert_element_type.61, f32[384]{0:T(512)S(1)} %rsqrt_reduce_fusion), kind=kOutput, calls=%fused_computation.5 | convolution fusion | flops 2521006080 | bytes 9514496 | tf_op jit(solution)/shard_map/dot_general | solution.py:482
  20.3 1.2 pad_maximum_fusion
  21.6 0.6 reshape.105.gain_ref
  22.2 0.3 multiply_cosine_fusion
  22.6 0.1 copy.25
  22.7 7.1 %reduce-scatter.2.cloned.1.call-done = bf16[192,1792]{1,0:T(8,128)(2,1)} async-done(((bf16[384,1792]{1,0:T(8,128)(2,1)}), bf16[192,1792]{1,0:T(8,128)(2,1)}) %reduce-scatter.2.cloned.1.call-update) | async-done | bytes 688144 | tf_op jit(solution)/shard_map/reduce_scatter | solution.py:486
  29.9 1.2 convert_element_type.66
  31.2 0.1 reshape.98
  31.3 0.4 subtract_convert_fusion.1
  31.7 0.2 maximum_convert_fusion
  32.0 0.4 copy.23
  32.4 0.2 subtract_convert_fusion
  32.6 0.1 pad_maximum_fusion.1
  32.7 0.1 bitcast_convert_fusion
  32.9 0.4 copy.26.q_ref
  33.3 34.7 %attend.1 = (bf16[192,512,128]{2,1,0:T(8,128)(2,1)}, bf16[192,512,128]{2,1,0:T(8,128)(2,1)}, bf16[192,1280]{1,0:T(8,128)(2,1)S(1)}) custom-call(s32[192]{0:T(256)S(1)} %copy-done.1, f32[192,1280]{1,0:T(8,128)S(1)} %copy.26.q_ref, f32[192,256]{1,0:T(8,128)S(1)} %bitcast.15, f32[192,256]{1,0:T(8,128)S(1)} %get-tuple-element.11.vn_ref, ...), custom_call_target="tpu_custom_call" | custom-call | tf_op jit(solution)/shard_map/attend/pallas_call | solution.py:125
  68.0 0.8 copy-done
  68.8 105.8 %tail.1 = bf16[384,2560]{1,0:T(8,128)(2,1)} custom-call(bf16[192,1280]{1,0:T(8,128)(2,1)} %copy-done, bf16[384,2560]{1,0:T(8,128)(2,1)} %x_hbm.1, f32[1,2560]{1,0:T(1,128)} %reshape.105.gain_ref, bf16[1280,2560]{1,0:T(8,128)(2,1)} %wo_hbm.1, bf16[2560,3456]{1,0:T(8,128)(2,1)} %wg_hbm.1, bf16[2560,3456]{1,0:T(8,128)(2,1)} %wu_hbm.1, bf16[3456,2560]{1,0:T(8,128)(2,1)} %wd_hbm.1), custom_call_target="tpu_custom_call" | custom-call | tf_op jit(solution)/shard_map/tail/pallas_call | solution.py:426
  174.6 2.9 %copy.33 = bf16[384,2560]{1,0:T(8,128)(2,1)} copy(bf16[384,2560]{1,0:T(8,128)(2,1)} %tail.1) | data formatting | bytes 3932160
  (32 shorter events, 0.4 us)
Async XLA Ops:
  7.2 5.3 %copy-start.2 = (bf16[384,2560]{1,0:T(8,128)(2,1)S(1)}, bf16[384,2560]{1,0:T(8,128)(2,1)}, u32[]{:S(2)}) copy-start(bf16[384,2560]{1,0:T(8,128)(2,1)} %x_hbm.1) | copy-start | bytes 5898244
  7.2 5.2 %copy-start.3 = (bf16[2560]{0:T(1024)(128)(2,1)S(1)}, bf16[2560]{0:T(1024)(128)(2,1)}, u32[]{:S(2)}) copy-start(bf16[2560]{0:T(1024)(128)(2,1)} %param.18) | copy-start | bytes 15364
  7.2 22.7 %reduce-scatter.2.cloned.1.call-start = ((), (), s32[]{:S(2)}) async-start(), calls=%async_computation.1 | async-start | bytes 2064384 | tf_op jit(solution)/shard_map/reduce_scatter | solution.py:486
  12.4 2.2 %copy-start.7 = (bf16[2560,256]{1,0:T(8,128)(2,1)S(1)}, bf16[2560,256]{1,0:T(8,128)(2,1)}, u32[]{:S(2)}) copy-start(bf16[2560,256]{1,0:T(8,128)(2,1)} %param.24) | copy-start | bytes 3932164
  14.6 2.9 %copy-start.6 = (bf16[2560,1280]{1,0:T(8,128)(2,1)S(1)}, bf16[2560,1280]{1,0:T(8,128)(2,1)}, u32[]{:S(2)}) copy-start(bf16[2560,1280]{1,0:T(8,128)(2,1)} %param.20) | copy-start | bytes 19660804
  20.2 1.3 copy-start.8
  20.2 1.3 copy-start.9
  20.3 1.3 copy-start.1
  20.3 1.3 copy-start.5
  20.3 1.3 copy-start.4
  68.0 0.8 copy-start
Sparse Core Ops, SparseCore 0:
  21.6 8.2 reduce-scatter.1

commit v3 on v2

--- a/solution.py
+++ b/solution.py
@@ -1,5 +1,6 @@
 import jax
 import jax.numpy as jnp
+import numpy as np
 from jax import lax
 from jax.experimental import pallas as pl
 from jax.experimental.pallas import tpu as pltpu
@@ -21,7 +22,7 @@
 MESH = pl.DeviceIdType.MESH
 
 
-def attend_kernel(lens, q_ref, kn_ref, vn_ref, kc, vc, ko, vo, out_ref, kbuf, vbuf, qs, os, sems):
+def attend_kernel(lens, q_hbm, kn_hbm, vn_hbm, kc, vc, ko, vo, out_hbm, kbuf, vbuf, q_ref, kn_ref, vn_ref, out_ref, qs, os, sems, in_sem, out_sem):
     rows = q_ref.shape[0]
     heads = q_ref.shape[1] // HEAD
     flat = kbuf.shape[2]
@@ -38,7 +39,14 @@
     for block in range(AHEAD):
         for move in moves(block, block, True):
             move.start()
+    loads = [pltpu.make_async_copy(src, dst, in_sem.at[i]) for i, (src, dst) in enumerate(((q_hbm, q_ref), (kn_hbm, kn_ref), (vn_hbm, vn_ref)))]
+    for load in loads:
+        load.start()
     qs[...] = jnp.zeros_like(qs)
+
+    def put_out(step):
+        part = pl.ds(pl.multiple_of(step * 16, 16), 16)
+        return pltpu.make_async_copy(out_ref.at[part], out_hbm.at[part], out_sem)
 
     tile_row = lax.broadcasted_iota(jnp.int32, (PAD_HEADS, HEAD), 0)
     pair_row = lax.broadcasted_iota(jnp.int32, (2 * PAD_HEADS, flat), 0)
@@ -56,6 +64,9 @@
         other = jnp.broadcast_to(new8[j:j + 1, HEAD:], (16, HEAD)).astype(jnp.bfloat16)
         tile = jnp.where(tile_row == off, first, jnp.where(tile_row == off + 1, other, tile))
         buf[slot, j, pl.ds(base, 16), :] = tile
+
+    for load in loads:
+        load.wait()
 
     @pl.loop(0, blocks // 2)
     def _(step):
@@ -110,6 +121,12 @@
         for h in range(heads):
             out_ref[pl.ds(pl.multiple_of(step * 16, 16), 16), h * HEAD:(h + 1) * HEAD] = os[pl.ds(h, 16, stride=PAD_HEADS), :].astype(jnp.bfloat16)
 
+        @pl.when(step > 0)
+        def _():
+            put_out(step - 1).wait()
+        put_out(step).start()
+
+    put_out(blocks // 2 - 1).wait()
     for block in range(blocks - SLOTS, blocks):
         for move in moves(block, block % SLOTS, False):
             move.wait()
@@ -120,29 +137,34 @@
     flat = seq * kv
     kc = k_cache.reshape(rows, flat, HEAD)
     vc = v_cache.reshape(rows, flat, HEAD)
-    whole = pl.BlockSpec(memory_space=pltpu.VMEM)
     hbm = pl.BlockSpec(memory_space=pltpu.HBM)
     ko, vo, out = pl.pallas_call(
         attend_kernel,
         out_shape=(jax.ShapeDtypeStruct(kc.shape, kc.dtype), jax.ShapeDtypeStruct(vc.shape, vc.dtype), jax.ShapeDtypeStruct(q.shape, jnp.bfloat16)),
-        in_specs=[pl.BlockSpec(memory_space=pltpu.SMEM), whole, whole, whole, hbm, hbm],
-        out_specs=(hbm, hbm, whole),
+        in_specs=[pl.BlockSpec(memory_space=pltpu.SMEM)] + [hbm] * 5,
+        out_specs=(hbm, hbm, hbm),
         scratch_shapes=[
             pltpu.VMEM((SLOTS, SLOT_ROWS, flat, HEAD), jnp.bfloat16),
             pltpu.VMEM((SLOTS, SLOT_ROWS, flat, HEAD), jnp.bfloat16),
+            pltpu.VMEM(q.shape, q.dtype),
+            pltpu.VMEM(k_new.shape, k_new.dtype),
+            pltpu.VMEM(v_new.shape, v_new.dtype),
+            pltpu.VMEM(q.shape, jnp.bfloat16),
             pltpu.VMEM((SLOT_ROWS * PAD_HEADS, HEAD), jnp.float32),
             pltpu.VMEM((2 * SLOT_ROWS * PAD_HEADS, HEAD), jnp.float32),
             pltpu.SemaphoreType.DMA((4, SLOTS)),
+            pltpu.SemaphoreType.DMA((3,)),
+            pltpu.SemaphoreType.DMA(()),
         ],
-        compiler_params=pltpu.CompilerParams(vmem_limit_bytes=40 << 20),
+        compiler_params=pltpu.CompilerParams(vmem_limit_bytes=67043328),
         name="attend",
     )(lens, q, k_new, v_new, kc, vc)
     return ko.reshape(k_cache.shape), vo.reshape(v_cache.shape), out
 
 
-def tail_kernel(attn_ref, x_hbm, gain_ref, wo_hbm, wg_hbm, wu_hbm, wd_hbm, out_ref,
+def tail_kernel(attn_hbm, x_hbm, gain_ref, wo_hbm, wg_hbm, wu_hbm, wd_hbm, out_ref,
                 attn_all, xown, wo_v, wd_v, ring, sb, rb, keep, mall, hbuf, gsend, grecv, act, ssq, ssr,
-                wo_sem, wd_sem, ring_sem, x_sem, ici_ss, ici_rs, gu_ss, gu_rs, act_ss, act_rs, st_ss, st_rs, at_ss, at_rs):
+                wo_sem, wd_sem, ring_sem, x_sem, ici_ss, ici_rs, gu_ss, gu_rs, act_ss, act_rs, st_ss, st_rs, at_ss, at_rs, at_sem):
     my, mx = lax.axis_index("my"), lax.axis_index("mx")
     row_count, hidden = out_ref.shape
     half_rows = row_count // 2
@@ -171,6 +193,8 @@
     for peer in (device(1), device(2), partner):
         pl.semaphore_signal(barrier, inc=1, device_id=peer, device_id_type=MESH)
 
+    attn_copy = pltpu.make_async_copy(attn_hbm, attn_all.at[mx], at_sem)
+    attn_copy.start()
     order = (3, 1, 2, 0)
     wo_copies = {r: pltpu.make_async_copy(wo_hbm.at[:, cols(r)], wo_v.at[r], wo_sem.at[r]) for r in order}
     wd_copies = {r: pltpu.make_async_copy(wd_hbm.at[:, cols(r)], wd_v.at[r], wd_sem.at[r]) for r in order}
@@ -194,18 +218,15 @@
     def hop(c, s, msg, src, dst, r):
         return remote(src, dst, ici_ss.at[c, s, msg], ici_rs.at[c, s, msg], device(r))
 
+    attn_copy.wait()
     pl.semaphore_wait(barrier, 3)
-    attn_msg = remote(attn_ref, attn_all.at[mx], at_ss, at_rs, partner)
+    attn_msg = remote(attn_all.at[mx], attn_all.at[mx], at_ss, at_rs, partner)
     attn_msg.start()
 
     def for_rows(count, body):
         @pl.loop(0, count // ROWS_STEP)
         def _(i):
             body(pl.multiple_of(i * ROWS_STEP, ROWS_STEP))
-
-    def copy_attn(at):
-        attn_all[mx, pl.ds(at, ROWS_STEP), :] = attn_ref[pl.ds(at, ROWS_STEP), :]
-    for_rows(half_rows, copy_attn)
 
     def rs_msg(c, s, base, k):
         return hop(c, s, base + k, sb.at[c, s, k], rb.at[c, s, k], second(s) if k == 2 else first(s))
@@ -318,8 +339,10 @@
             total = jnp.sum(ssq[c, rows, :] + ssr[c, rows, :], axis=1, keepdims=True)
             inv = lax.rsqrt(total / (2 * hidden) + NORM_EPS)
             for j in range(4):
-                at_col = slice(j * PIECE, (j + 1) * PIECE)
-                hbuf[rows, at_col] = (mall[c, j, rows, :].astype(jnp.float32) * inv * gain_ref[:, at_col]).astype(jnp.bfloat16)
+                for k in range(PIECE // 128):
+                    tile = j * (PIECE // 128) + k
+                    m = mall[c, j, rows, k * 128:(k + 1) * 128].astype(jnp.float32)
+                    hbuf[rows, tile * 128:(tile + 1) * 128] = (m * inv * gain_ref[tile:tile + 1, :].astype(jnp.float32)).astype(jnp.bfloat16)
         for_rows(2 * sub, scale)
 
     def gu_msg(c, t):
@@ -426,7 +449,7 @@
     return pl.pallas_call(
         tail_kernel,
         out_shape=jax.ShapeDtypeStruct((rows, hidden), bf16),
-        in_specs=[whole, hbm, whole, hbm, hbm, hbm, hbm],
+        in_specs=[hbm, hbm, whole, hbm, hbm, hbm, hbm],
         out_specs=whole,
         scratch_shapes=[
             pltpu.VMEM((2, rows // 2, q_width), bf16),
@@ -449,53 +472,157 @@
             dma((CHUNKS, steps)), dma((CHUNKS, steps)),
             dma((CHUNKS, 2)), dma((CHUNKS, 2)),
             dma((CHUNKS,)), dma((CHUNKS,)),
-            dma(()), dma(()),
+            dma(()), dma(()), dma(()),
         ],
         compiler_params=pltpu.CompilerParams(collective_id=1, has_side_effects=True, vmem_limit_bytes=67043328),
         name="tail",
     )(attn, x_in, gain, w_o, w_gate, w_up, w_down)
 
 
-def rotate(cols, cos_tab, sin_tab):
-    rows, width = cols.shape
-    heads = cols.reshape(rows, width // HEAD, HEAD)
-    lower, upper = heads[..., :HEAD // 2], heads[..., HEAD // 2:]
-    out = jnp.concatenate([lower * cos_tab - upper * sin_tab, upper * cos_tab + lower * sin_tab], axis=-1)
-    return out.astype(jnp.bfloat16).astype(jnp.float32).reshape(rows, width)
+def head_kernel(x_hbm, gain_ref, bq_ref, bk_ref, bv_ref, cos_ref, sin_ref, wq_hbm, wk_hbm, wv_hbm, q_out, k_out, v_out,
+                xv, wv_all, hbuf, keep, psend, precv, ssq, ssr, x_sem, w_sem, st_ss, st_rs, p_ss, p_rs):
+    my, mx = lax.axis_index("my"), lax.axis_index("mx")
+    rows, hidden = xv.shape
+    half = rows // 2
+    q_cols, kv_cols = wq_hbm.shape[1], wk_hbm.shape[1]
+    width = q_cols + 2 * kv_cols
+    partner = (my, 1 - mx)
+    barrier = pltpu.get_barrier_semaphore()
+    pl.semaphore_signal(barrier, inc=1, device_id=partner, device_id_type=MESH)
+
+    x_parts = 4
+    x_rows = rows // x_parts
+    x_copies = [pltpu.make_async_copy(x_hbm.at[pl.ds(i * x_rows, x_rows)], xv.at[pl.ds(i * x_rows, x_rows)], x_sem.at[i]) for i in range(x_parts)]
+    w_copies = [
+        pltpu.make_async_copy(wq_hbm, wv_all.at[:, pl.ds(0, q_cols)], w_sem.at[0]),
+        pltpu.make_async_copy(wk_hbm, wv_all.at[:, pl.ds(q_cols, kv_cols)], w_sem.at[1]),
+        pltpu.make_async_copy(wv_hbm, wv_all.at[:, pl.ds(q_cols + kv_cols, kv_cols)], w_sem.at[2]),
+    ]
+    for copy in x_copies + w_copies:
+        copy.start()
+
+    def remote(src, dst, ss, rs):
+        return pltpu.make_async_remote_copy(src_ref=src, dst_ref=dst, send_sem=ss, recv_sem=rs, device_id=partner, device_id_type=MESH)
+
+    for i in range(x_parts):
+        x_copies[i].wait()
+
+        @pl.loop(0, x_rows // ROWS_STEP)
+        def _(step, i=i):
+            at = pl.ds(pl.multiple_of(i * x_rows + step * ROWS_STEP, ROWS_STEP), ROWS_STEP)
+            total = jnp.zeros((ROWS_STEP, 128), jnp.float32)
+            for k in range(0, hidden, 128):
+                m = xv[at, k:k + 128].astype(jnp.float32)
+                total = total + m * m
+            ssq[at, :] = total
+    pl.semaphore_wait(barrier, 1)
+    stats = remote(ssq, ssr, st_ss, st_rs)
+    stats.start()
+    stats.wait()
+
+    def normalise(start):
+        @pl.loop(0, half // ROWS_STEP)
+        def _(step):
+            at = pl.ds(pl.multiple_of(start + step * ROWS_STEP, ROWS_STEP), ROWS_STEP)
+            total = jnp.sum(ssq[at, :] + ssr[at, :], axis=1, keepdims=True)
+            inv = lax.rsqrt(total / (2 * hidden) + NORM_EPS)
+            for k in range(hidden // 128):
+                lanes = slice(k * 128, (k + 1) * 128)
+                hbuf[at, lanes] = (xv[at, lanes].astype(jnp.float32) * inv * gain_ref[k:k + 1, :].astype(jnp.float32)).astype(jnp.bfloat16)
+
+    theirs = pl.multiple_of((1 - mx) * half, half)
+    mine = pl.multiple_of(mx * half, half)
+    normalise(theirs)
+    for copy in w_copies:
+        copy.wait()
+    spans = [(lo, min(lo + 512, width)) for lo in range(0, width, 512)]
+
+    def piece(i, lo, hi):
+        return remote(psend.at[:, pl.ds(lo, hi - lo)], precv.at[:, pl.ds(lo, hi - lo)], p_ss.at[i], p_rs.at[i])
+
+    for i, (lo, hi) in enumerate(spans):
+        psend[:, lo:hi] = jnp.dot(hbuf[pl.ds(theirs, half), :], wv_all[:, lo:hi], preferred_element_type=jnp.float32).astype(jnp.bfloat16)
+        piece(i, lo, hi).start()
+    normalise(mine)
+    for i, (lo, hi) in enumerate(spans):
+        keep[:, lo:hi] = jnp.dot(hbuf[pl.ds(mine, half), :], wv_all[:, lo:hi], preferred_element_type=jnp.float32)
+    for i, (lo, hi) in enumerate(spans):
+        piece(i, lo, hi).wait_recv()
+
+    def bias_row(ref, h):
+        return ref[h:h + 1, :].astype(jnp.float32)
+
+    @pl.loop(0, half // ROWS_STEP)
+    def _(step):
+        at = pl.ds(pl.multiple_of(step * ROWS_STEP, ROWS_STEP), ROWS_STEP)
+        cos_tab, sin_tab = cos_ref[at, :], sin_ref[at, :]
+        for h in range(width // HEAD):
+            lanes = slice(h * HEAD, (h + 1) * HEAD)
+            vals = keep[at, lanes] + precv[at, lanes].astype(jnp.float32)
+            if h < q_cols // HEAD:
+                out, ref, j, spin = q_out, bq_ref, h, True
+            elif h < (q_cols + kv_cols) // HEAD:
+                out, ref, j, spin = k_out, bk_ref, h - q_cols // HEAD, True
+            else:
+                out, ref, j, spin = v_out, bv_ref, h - (q_cols + kv_cols) // HEAD, False
+            vals = vals + bias_row(ref, j)
+            if spin:
+                vals = vals * cos_tab + pltpu.roll(vals, HEAD // 2, 1) * sin_tab
+            out[at, j * HEAD:(j + 1) * HEAD] = vals.astype(jnp.bfloat16).astype(jnp.float32)
+
+    for i, (lo, hi) in enumerate(spans):
+        piece(i, lo, hi).wait_send()
+
+
+def head(x_in, gain, b_q, b_k, b_v, cos_tab, sin_tab, w_q, w_k, w_v):
+    rows, hidden = x_in.shape
+    half = rows // 2
+    q_cols, kv_cols = w_q.shape[1], w_k.shape[1]
+    width = q_cols + 2 * kv_cols
+    whole = pl.BlockSpec(memory_space=pltpu.VMEM)
+    hbm = pl.BlockSpec(memory_space=pltpu.HBM)
+    bf16, f32 = jnp.bfloat16, jnp.float32
+    dma = pltpu.SemaphoreType.DMA
+    return pl.pallas_call(
+        head_kernel,
+        out_shape=(jax.ShapeDtypeStruct((half, q_cols), f32), jax.ShapeDtypeStruct((half, kv_cols), f32), jax.ShapeDtypeStruct((half, kv_cols), f32)),
+        in_specs=[hbm] + [whole] * 6 + [hbm] * 3,
+        out_specs=(whole, whole, whole),
+        scratch_shapes=[
+            pltpu.VMEM((rows, hidden), bf16),
+            pltpu.VMEM((hidden, width), bf16),
+            pltpu.VMEM((rows, hidden), bf16),
+            pltpu.VMEM((half, width), f32),
+            pltpu.VMEM((half, width), bf16),
+            pltpu.VMEM((half, width), bf16),
+            pltpu.VMEM((rows, 128), f32),
+            pltpu.VMEM((rows, 128), f32),
+            dma((4,)), dma((3,)), dma(()), dma(()), dma((4,)), dma((4,)),
+        ],
+        compiler_params=pltpu.CompilerParams(collective_id=0, has_side_effects=True, vmem_limit_bytes=67043328),
+        name="head",
+    )(x_in, gain, b_q, b_k, b_v, cos_tab, sin_tab, w_q, w_k, w_v)
+
+
+def lanes_of(vec):
+    return vec.reshape(-1, 128)
 
 
 def solution(mesh):
-    mx_size = mesh.shape["mx"]
     act_spec = P(None, "mx")
     cache_spec = P("mx", None, "my", None)
     in_specs = (act_spec, P("mx"), P("mx"), P("mx"), P("mx", "my"), P("my"), P("mx", "my"), P("my"), P("mx", "my"), P("my"), P("my", "mx"), P("mx", "my"), P("mx", "my"), P("my", "mx"), cache_spec, cache_spec)
     out_specs = (act_spec, cache_spec, cache_spec)
 
     def local_layer(x_in, seq_lens, gain_attn, gain_mlp, w_q, b_q, w_k, b_k, w_v, b_v, w_o, w_gate, w_up, w_down, k_cache, v_cache):
-        hidden = x_in.shape[1] * mx_size
-        x_f32 = x_in.astype(jnp.float32)
-        attn_sq = lax.psum(jnp.sum(x_f32 * x_f32, axis=1, keepdims=True), "mx")
-        normed = (x_f32 * lax.rsqrt(attn_sq / hidden + NORM_EPS) * gain_attn.astype(jnp.float32)).astype(jnp.bfloat16)
-        q_cols = w_q.shape[1]
-        kv_cols = w_k.shape[1]
-        partials = jnp.concatenate([
-            jnp.dot(normed, w_q, preferred_element_type=jnp.float32).astype(jnp.bfloat16),
-            jnp.dot(normed, w_k, preferred_element_type=jnp.float32).astype(jnp.bfloat16),
-            jnp.dot(normed, w_v, preferred_element_type=jnp.float32).astype(jnp.bfloat16),
-        ], axis=1)
-        projected = lax.psum_scatter(partials, "mx", scatter_dimension=0, tiled=True).astype(jnp.float32)
-        q_vals = projected[:, :q_cols] + b_q.astype(jnp.float32)
-        k_vals = projected[:, q_cols:q_cols + kv_cols] + b_k.astype(jnp.float32)
-        v_vals = projected[:, q_cols + kv_cols:] + b_v.astype(jnp.float32)
         half_dim = HEAD // 2
-        inv_freq = ROPE_THETA ** (-2.0 * jnp.arange(half_dim, dtype=jnp.float32) / HEAD)
-        angles = seq_lens.astype(jnp.float32)[:, None, None] * inv_freq
-        cos_tab, sin_tab = jnp.cos(angles), jnp.sin(angles)
-        q_rot = rotate(q_vals, cos_tab, sin_tab)
-        k_rot = rotate(k_vals, cos_tab, sin_tab)
-        v_new = v_vals.astype(jnp.bfloat16).astype(jnp.float32)
+        inv_freq = (ROPE_THETA ** (-2.0 * (np.arange(HEAD) % half_dim) / HEAD)).astype(np.float32)
+        sign = np.where(np.arange(HEAD) < half_dim, -1.0, 1.0).astype(np.float32)
+        angles = seq_lens.astype(jnp.float32)[:, None] * inv_freq
+        cos_tab, sin_tab = jnp.cos(angles), jnp.sin(angles) * sign
+        q_rot, k_rot, v_new = head(x_in, lanes_of(gain_attn), lanes_of(b_q), lanes_of(b_k), lanes_of(b_v), cos_tab, sin_tab, w_q, w_k, w_v)
         k_cache_out, v_cache_out, attn_rows = attend(seq_lens, q_rot, k_rot, v_new, k_cache, v_cache)
-        x_out = tail(attn_rows, x_in, gain_mlp.astype(jnp.float32)[None, :], w_o, w_gate, w_up, w_down)
+        x_out = tail(attn_rows, x_in, lanes_of(gain_mlp), w_o, w_gate, w_up, w_down)
         return x_out, k_cache_out, v_cache_out
 
     return jax.shard_map(local_layer, mesh=mesh, in_specs=in_specs, out_specs=out_specs, check_vma=False)

time: 185 us -> 166 us (0.90)
  Pallas kernels: 141 us -> 160 us
  between operations: 14.4 us -> 0.65 us
  waiting for transfers between devices: 7.16 us -> 0 us
  matrix products: 5.64 us -> 0 us
  local copies, waits for them, and re-layouts: 7.56 us -> 2.94 us
  other arithmetic: 6.1 us -> 2.46 us
  blocking collectives: 2.99 us -> 0 us
    pallas_call x0 -> x1, Pallas kernels: none -> 16.7 us  [head(): pl.pallas_call(head_kernel, out_shape=(jax.ShapeDtypeStruct((half, q_cols...]
    reduce_scatter x1 -> x0, waiting for transfers between devices: 7.15 us -> none  [local_layer(): lax.psum_scatter(partials, 'mx', scatter_dimension=0, tiled=True)]
    dot_general x3 -> x0, matrix products: 5.64 us -> none  [the longest x1 2.75 us: local_layer(): jnp.dot(normed, w_q, preferred_element_type=jnp.float32)]
    psum x1 -> x0, blocking collectives: 2.99 us -> none  [local_layer(): attn_sq = lax.psum(jnp.sum(x_f32 * x_f32, axis=1, keepdims=True), 'mx')]
    unnamed x22 -> x1, local copies, waits for them, and re-layouts: 5.88 us -> 2.94 us
    reduce_sum x1 -> x0, other arithmetic: 2.14 us -> none  [local_layer(): attn_sq = lax.psum(jnp.sum(x_f32 * x_f32, axis=1, keepdims=True), 'mx')]
  transfers between devices with their start and end apart: 1 -> 0, of which waited for: 1 -> 0; matrix products, arithmetic and copies ran while one was open for 1% -> 0% of each run, Pallas kernels for 0% -> 0%
where the time goes in v3:
time: 166 us
  Pallas kernels  160 us (96%)
  local copies, waits for them, and re-layouts  2.94 us (2%)
  other arithmetic  2.46 us (1%)
    pallas_call x1, Pallas kernels, tail(): pl.pallas_call(tail_kernel, out_shape=jax.ShapeDtypeStruct((rows, hidden)...  107 us
    pallas_call x1, Pallas kernels, attend(): pl.pallas_call(attend_kernel, out_shape=(jax.ShapeDtypeStruct(kc.shape, k...  36.1 us
    pallas_call x1, Pallas kernels, head(): pl.pallas_call(head_kernel, out_shape=(jax.ShapeDtypeStruct((half, q_cols...  16.7 us

profile of v3, /device:TPU:0, one launch (start us, length us, event | category | flops | bytes accessed | tf_op | source)
XLA Modules:
  0.0 166.1 jit_solution(17285586915747717397)
XLA Ops:
  0.6 0.7 convert_element_type.3
  1.3 1.8 %fusion = (f32[192,128]{1,0:T(8,128)}, f32[192,128]{1,0:T(8,128)}) fusion(f32[128]{0:T(128)} %constant.5.clone, f32[128]{0:T(128)} %constant.4.clone, f32[192]{0:T(256)S(1)} %convert_element_type.3), kind=kLoop, calls=%fused_computation.2 | loop fusion | flops 49152 | bytes 198400 | tf_op jit(solution)/shard_map/mul | solution.py:622
  3.1 16.7 %head.1 = (f32[192,1280]{1,0:T(8,128)}, f32[192,256]{1,0:T(8,128)}, f32[192,256]{1,0:T(8,128)}) custom-call(bf16[384,2560]{1,0:T(8,128)(2,1)} %x_hbm.3, bf16[20,128]{1,0:T(8,128)(2,1)} %bitcast.11, bf16[10,128]{1,0:T(8,128)(2,1)} %bitcast.13, bf16[2,128]{1,0:T(2,128)(2,1)} %bitcast.14, bf16[2,128]{1,0:T(2,128)(2,1)} %bitcast.15, ...), custom_call_target="tpu_custom_call" | custom-call | tf_op jit(solution)/shard_map/head/pallas_call | solution.py:586
  19.7 36.1 %attend.1 = (bf16[192,512,128]{2,1,0:T(8,128)(2,1)}, bf16[192,512,128]{2,1,0:T(8,128)(2,1)}, bf16[192,1280]{1,0:T(8,128)(2,1)}) custom-call(s32[192]{0:T(256)} %lens.1, f32[192,1280]{1,0:T(8,128)} %get-tuple-element.9.q_hbm, f32[192,256]{1,0:T(8,128)} %get-tuple-element.10.kn_hbm, f32[192,256]{1,0:T(8,128)} %get-tuple-element.11.vn_hbm, ...), custom_call_target="tpu_custom_call" | custom-call | tf_op jit(solution)/shard_map/attend/pallas_call | solution.py:141
  55.9 107.3 %tail.1 = bf16[384,2560]{1,0:T(8,128)(2,1)} custom-call(bf16[192,1280]{1,0:T(8,128)(2,1)} %get-tuple-element.12.attn_hbm, bf16[384,2560]{1,0:T(8,128)(2,1)} %x_hbm.3, bf16[20,128]{1,0:T(8,128)(2,1)} %bitcast.12, bf16[1280,2560]{1,0:T(8,128)(2,1)} %wo_hbm.1, bf16[2560,3456]{1,0:T(8,128)(2,1)} %wg_hbm.1, bf16[2560,3456]{1,0:T(8,128)(2,1)} %wu_hbm.1, ...), custom_call_target="tpu_custom_call" | custom-call | tf_op jit(solution)/shard_map/tail/pallas_call | solution.py:449
  163.2 2.9 %copy.22 = bf16[384,2560]{1,0:T(8,128)(2,1)} copy(bf16[384,2560]{1,0:T(8,128)(2,1)} %tail.1) | data formatting | bytes 3932160

commit v4 on v3

--- a/solution.py
+++ b/solution.py
@@ -13,12 +13,14 @@
 SLOTS = 8
 AHEAD = 6
 PAD_HEADS = 16
-CHUNKS = 1
-RING = 6
+CHUNKS = 2
+RING = 8
 PIECE = 640
 TILE = 256
-MROWS = 192
 ROWS_STEP = 16
+NORM_ROWS = 64
+SERVE = ((5, 11), (9, 14))
+HEAD_ROWS = 48
 MESH = pl.DeviceIdType.MESH
 
 
@@ -196,8 +198,8 @@
     attn_copy = pltpu.make_async_copy(attn_hbm, attn_all.at[mx], at_sem)
     attn_copy.start()
     order = (3, 1, 2, 0)
-    wo_copies = {r: pltpu.make_async_copy(wo_hbm.at[:, cols(r)], wo_v.at[r], wo_sem.at[r]) for r in order}
-    wd_copies = {r: pltpu.make_async_copy(wd_hbm.at[:, cols(r)], wd_v.at[r], wd_sem.at[r]) for r in order}
+    wo_copies = {r: pltpu.make_async_copy(wo_hbm.at[:, cols(r)], wo_v.at[:, pl.ds(i * PIECE, PIECE)], wo_sem.at[r]) for i, r in enumerate(order)}
+    wd_copies = {r: pltpu.make_async_copy(wd_hbm.at[:, cols(r)], wd_v.at[:, pl.ds(i * PIECE, PIECE)], wd_sem.at[r]) for i, r in enumerate(order)}
     x_copy = pltpu.make_async_copy(x_hbm.at[:, cols(0)], xown, x_sem)
     for r in order:
         wo_copies[r].start()
@@ -223,119 +225,133 @@
     attn_msg = remote(attn_all.at[mx], attn_all.at[mx], at_ss, at_rs, partner)
     attn_msg.start()
 
-    def for_rows(count, body):
-        @pl.loop(0, count // ROWS_STEP)
+    def for_rows(count, body, step=ROWS_STEP):
+        @pl.loop(0, count // step)
         def _(i):
-            body(pl.multiple_of(i * ROWS_STEP, ROWS_STEP))
+            body(pl.multiple_of(i * step, step))
+
+    part = sub // 2
 
     def rs_msg(c, s, base, k):
-        return hop(c, s, base + k, sb.at[c, s, k], rb.at[c, s, k], second(s) if k == 2 else first(s))
-
-    blocks = 2 * sub // MROWS
-
-    def parts(block):
-        if CHUNKS == 1:
-            return ((block, 0, sub),)
-        return ((0, 0, sub), (1, sub, 2 * sub))
-
-    def product(c, r, lhs, weights, base, send):
-        for block in range(blocks):
-            acc = jnp.dot(lhs(block), weights[...], preferred_element_type=jnp.float32)
-            for s, lo, hi in parts(block):
-                piece = acc[lo:hi]
-                if r == 3 or r == first(s):
-                    which = 0 if r == 3 else 1
-                    sb[c, s, which] = piece.astype(jnp.bfloat16)
-                    if send:
-                        rs_msg(c, s, base, which).start()
-                else:
-                    keep[c, s, 0 if r == second(s) else 1] = piece
-
-    def rs_send(c, base):
-        for which in range(2):
+        if k < 2:
+            return hop(c, s, base + k, sb.at[c, s, k], rb.at[c, s, k], first(s))
+        rows = pl.ds((k - 2) * part, part)
+        return hop(c, s, base + k, sb.at[c, s, 2, rows], rb.at[c, s, 2, rows], second(s))
+
+    def product(c, lhs, weights, copies, base, send):
+        waited = []
+        for lo in range(0, hidden, 2 * TILE):
+            hi = lo + 2 * TILE
+            held = [(i, order[i]) for i in range(4) if i * PIECE < hi and (i + 1) * PIECE > lo]
+            for _, r in held:
+                if copies and r not in waited:
+                    waited.append(r)
+                    copies[r].wait()
+            acc = jnp.dot(lhs, weights[:, lo:hi], preferred_element_type=jnp.float32)
+            for i, r in held:
+                left, right = max(lo, i * PIECE), min(hi, (i + 1) * PIECE)
+                where = slice(left - i * PIECE, right - i * PIECE)
+                for s in range(2):
+                    piece = acc[s * sub:(s + 1) * sub, left - lo:right - lo]
+                    if r == 3 or r == first(s):
+                        which = 0 if r == 3 else 1
+                        sb[c, s, which, :, where] = piece.astype(jnp.bfloat16)
+                        if send and right == (i + 1) * PIECE:
+                            rs_msg(c, s, base, which).start()
+                    else:
+                        keep[c, s, 0 if r == second(s) else 1, :, where] = piece
+
+    def rs_middle(c, base):
+        for k in range(2):
             for s in range(2):
-                rs_msg(c, s, base, which).start()
-
-    def rs_middle(c, base):
-        for s in range(2):
-            rs_msg(c, s, base, 0).wait_recv()
-
-            def add(at, s=s):
-                rows = pl.ds(at, ROWS_STEP)
-                sb[c, s, 2, rows, :] = (keep[c, s, 0, rows, :] + rb[c, s, 0, rows, :].astype(jnp.float32)).astype(jnp.bfloat16)
-            for_rows(sub, add)
-            rs_msg(c, s, base, 2).start()
-
-    def rs_sum(c, s, rows):
-        return keep[c, s, 1, rows, :] + rb[c, s, 1, rows, :].astype(jnp.float32) + rb[c, s, 2, rows, :].astype(jnp.float32)
-
-    def mid_at(c, s, r):
-        return mall.at[c, chunk_of(r), pl.ds(s * sub, sub), :]
-
-    def out_at(c, s, r):
-        return out_ref.at[pl.ds(s * half_rows + c * sub, sub), cols(r)]
-
-    def ag_msg(c, s, base, at, k):
-        src = at(c, s, second(s) if k == 2 else 0)
-        return hop(c, s, base + k, src, src, second(s) if k == 0 else first(s))
+                if k == 0:
+                    rs_msg(c, s, base, 0).wait_recv()
+
+                def add(at, s=s, k=k):
+                    rows = pl.ds(k * part + at, ROWS_STEP)
+                    sb[c, s, 2, rows, :] = (keep[c, s, 0, rows, :] + rb[c, s, 0, rows, :].astype(jnp.float32)).astype(jnp.bfloat16)
+                for_rows(part, add)
+                rs_msg(c, s, base, 2 + k).start()
+
+    def mid_at(c, s, r, k):
+        return mall.at[c, chunk_of(r), pl.ds(s * sub + k * part, part), :]
+
+    def out_at(c, s, r, k):
+        return out_ref.at[pl.ds(s * half_rows + c * sub + k * part, part), cols(r)]
+
+    def ag_msg(c, s, base, at, j, k):
+        src = at(c, s, second(s) if j == 2 else 0, k)
+        return hop(c, s, base + 2 * j + k, src, src, second(s) if j == 0 else first(s))
+
+    def finish(c, base, store, at):
+        for k in range(2):
+            for s in range(2):
+                if k == 0:
+                    rs_msg(c, s, base, 1).wait_recv()
+                rs_msg(c, s, base, 2 + k).wait_recv()
+
+                def add(start, s=s, k=k):
+                    rows = pl.ds(k * part + start, ROWS_STEP)
+                    total = keep[c, s, 1, rows, :] + rb[c, s, 1, rows, :].astype(jnp.float32) + rb[c, s, 2, rows, :].astype(jnp.float32)
+                    store(c, s, k * part + start, total)
+                for_rows(part, add)
+                ag_msg(c, s, base + 4, at, 0, k).start()
+        for k in range(2):
+            for s in range(2):
+                ag_msg(c, s, base + 4, at, 1, k).start()
+
+    def store_mid(c, s, at, total):
+        total = total + xown[pl.ds(s * half_rows + c * sub + at, ROWS_STEP), :].astype(jnp.float32)
+        mall[c, my, pl.ds(s * sub + at, ROWS_STEP), :] = total.astype(jnp.bfloat16)
+
+    def store_out(c, s, at, total):
+        total = total + mall[c, my, pl.ds(s * sub + at, ROWS_STEP), :].astype(jnp.float32)
+        out_ref[pl.ds(s * half_rows + c * sub + at, ROWS_STEP), cols(0)] = total.astype(jnp.bfloat16)
 
     def finish_mid(c):
-        for s in range(2):
-            rs_msg(c, s, 0, 1).wait_recv()
-            rs_msg(c, s, 0, 2).wait_recv()
-
-            def add(at, s=s):
-                rows = pl.ds(at, ROWS_STEP)
-                total = rs_sum(c, s, rows) + xown[pl.ds(s * half_rows + c * sub + at, ROWS_STEP), :].astype(jnp.float32)
-                mall[c, my, pl.ds(s * sub + at, ROWS_STEP), :] = total.astype(jnp.bfloat16)
-            for_rows(sub, add)
-            ag_msg(c, s, 3, mid_at, 0).start()
-            ag_msg(c, s, 3, mid_at, 1).start()
+        finish(c, 0, store_mid, mid_at)
 
     def finish_out(c):
-        for s in range(2):
-            rs_msg(c, s, 6, 1).wait_recv()
-            rs_msg(c, s, 6, 2).wait_recv()
-
-            def add(at, s=s):
-                rows = pl.ds(at, ROWS_STEP)
-                total = rs_sum(c, s, rows) + mall[c, my, pl.ds(s * sub + at, ROWS_STEP), :].astype(jnp.float32)
-                out_ref[pl.ds(s * half_rows + c * sub + at, ROWS_STEP), cols(0)] = total.astype(jnp.bfloat16)
-            for_rows(sub, add)
-            ag_msg(c, s, 9, out_at, 0).start()
-            ag_msg(c, s, 9, out_at, 1).start()
+        finish(c, 10, store_out, out_at)
 
     def forward(c, base, at):
-        for s in range(2):
-            ag_msg(c, s, base, at, 0).wait_recv()
-            ag_msg(c, s, base, at, 2).start()
+        for k in range(2):
+            for s in range(2):
+                ag_msg(c, s, base, at, 0, k).wait_recv()
+                ag_msg(c, s, base, at, 2, k).start()
 
     def arrive(c, base, at):
         for s in range(2):
-            ag_msg(c, s, base, at, 1).wait_recv()
-            ag_msg(c, s, base, at, 2).wait_recv()
+            for k in range(2):
+                ag_msg(c, s, base, at, 1, k).wait_recv()
+                ag_msg(c, s, base, at, 2, k).wait_recv()
 
     def sent(c, base, at=None):
         for s in range(2):
-            for k in range(3):
-                (rs_msg(c, s, base, k) if at is None else ag_msg(c, s, base, at, k)).wait_send()
+            if at is None:
+                for k in range(4):
+                    rs_msg(c, s, base, k).wait_send()
+            else:
+                for j in range(3):
+                    for k in range(2):
+                        ag_msg(c, s, base, at, j, k).wait_send()
 
     def normalise(c):
         def squares(at):
-            rows = pl.ds(at, ROWS_STEP)
-            total = jnp.zeros((ROWS_STEP, 128), jnp.float32)
+            rows = pl.ds(at, NORM_ROWS)
+            total = jnp.zeros((NORM_ROWS, 128), jnp.float32)
             for j in range(4):
                 for k in range(0, PIECE, 128):
                     m = mall[c, j, rows, k:k + 128].astype(jnp.float32)
                     total = total + m * m
             ssq[c, rows, :] = total
-        for_rows(2 * sub, squares)
+        for_rows(2 * sub, squares, NORM_ROWS)
         msg = remote(ssq.at[c], ssr.at[c], st_ss.at[c], st_rs.at[c], partner)
         msg.start()
         msg.wait()
 
         def scale(at):
-            rows = pl.ds(at, ROWS_STEP)
+            rows = pl.ds(at, NORM_ROWS)
             total = jnp.sum(ssq[c, rows, :] + ssr[c, rows, :], axis=1, keepdims=True)
             inv = lax.rsqrt(total / (2 * hidden) + NORM_EPS)
             for j in range(4):
@@ -343,7 +359,7 @@
                     tile = j * (PIECE // 128) + k
                     m = mall[c, j, rows, k * 128:(k + 1) * 128].astype(jnp.float32)
                     hbuf[rows, tile * 128:(tile + 1) * 128] = (m * inv * gain_ref[tile:tile + 1, :].astype(jnp.float32)).astype(jnp.bfloat16)
-        for_rows(2 * sub, scale)
+        for_rows(2 * sub, scale, NORM_ROWS)
 
     def gu_msg(c, t):
         return remote(gsend.at[t], grecv.at[t], gu_ss.at[c, t], gu_rs.at[c, t], partner)
@@ -357,15 +373,13 @@
                 copy.wait()
             if mine:
                 gu_msg(c, t).wait_recv()
-            for block in range(blocks):
-                rows = slice(block * MROWS, (block + 1) * MROWS)
-                acc = jnp.dot(hbuf[rows, :], ring[slot], preferred_element_type=jnp.float32)
-                if mine:
-                    both = acc + grecv[t, rows, :].astype(jnp.float32)
-                    gate, up = both[:, :TILE], both[:, TILE:]
-                    act[rows, pl.ds(pl.multiple_of(mx * shift + t * TILE, 128), TILE)] = (gate * jax.nn.sigmoid(gate) * up).astype(jnp.bfloat16)
-                else:
-                    gsend[t, rows, :] = acc.astype(jnp.bfloat16)
+            acc = jnp.dot(hbuf[...], ring[slot], preferred_element_type=jnp.float32)
+            if mine:
+                both = acc + grecv[t].astype(jnp.float32)
+                gate, up = both[:, :TILE], both[:, TILE:]
+                act[:, pl.ds(pl.multiple_of(mx * shift + t * TILE, 128), TILE)] = (gate * jax.nn.sigmoid(gate) * up).astype(jnp.bfloat16)
+            else:
+                gsend[t] = acc.astype(jnp.bfloat16)
             if not mine:
                 gu_msg(c, t).start()
 
@@ -386,54 +400,70 @@
             gu_msg(c, t).wait_send()
 
     def attn_lhs(c):
-        def get(block):
-            if CHUNKS == 1:
-                return attn_all[block]
-            rows = slice(c * sub, (c + 1) * sub)
-            return jnp.concatenate([attn_all[0, rows, :], attn_all[1, rows, :]], axis=0)
-        return get
-
-    def act_lhs(block):
-        return act[block * MROWS:(block + 1) * MROWS, :]
+        rows = slice(c * sub, (c + 1) * sub)
+        return jnp.concatenate([attn_all[0, rows, :], attn_all[1, rows, :]], axis=0)
+
+    def mlp(c, at, early, late):
+        events = sorted([(at[0], 0, early), (at[1], 1, late), (steps + 4, 2, lambda: act_msg(c, 0).start()), (steps, 3, lambda: None), (per_chunk, 4, lambda: None)], key=lambda e: e[:2])
+        done = 0
+        for pos, _, act_on in events:
+            if pos > done:
+                mine = done // steps
+                tiles(c, mine, done - mine * steps, pos - mine * steps)
+                done = pos
+            act_on()
+        act_msg(c, 1).start()
 
     attn_msg.wait_recv()
-    for r in order:
-        wo_copies[r].wait()
-        if r == 3:
-            for g in range(RING):
-                for copy in ring_copies(g):
-                    copy.start()
-        product(0, r, attn_lhs(0), wo_v.at[r], 0, True)
+    product(0, attn_lhs(0), wo_v, wo_copies, 0, True)
+    for g in range(RING):
+        for copy in ring_copies(g):
+            copy.start()
+    product(1, attn_lhs(1), wo_v, {}, 0, False)
     x_copy.wait()
     for r in order:
         wd_copies[r].start()
     rs_middle(0, 0)
+    for s in range(2):
+        rs_msg(1, s, 0, 0).start()
     finish_mid(0)
-    forward(0, 3, mid_at)
-    arrive(0, 3, mid_at)
+    forward(0, 4, mid_at)
+    rs_middle(1, 0)
+    for s in range(2):
+        rs_msg(1, s, 0, 1).start()
+    arrive(0, 4, mid_at)
     normalise(0)
-    tiles(0, 0, 0, steps)
-    tiles(0, 1, 0, 4)
-    act_msg(0, 0).start()
-    tiles(0, 1, 4, steps)
-    act_msg(0, 1).start()
+    mlp(0, SERVE[0], lambda: finish_mid(1), lambda: forward(1, 4, mid_at))
     sent(0, 0)
     for k in range(2):
         act_msg(0, k).wait_recv()
-    for r in order:
-        wd_copies[r].wait()
-        product(0, r, act_lhs, wd_v.at[r], 6, True)
-    rs_middle(0, 6)
-    finish_out(0)
-    forward(0, 9, out_at)
-    arrive(0, 9, out_at)
+    product(0, act[...], wd_v, wd_copies, 10, True)
     gates_sent(0)
     for k in range(2):
         act_msg(0, k).wait_send()
-    sent(0, 3, mid_at)
-    sent(0, 6)
-    sent(0, 9, out_at)
+    arrive(1, 4, mid_at)
+    normalise(1)
+    rs_middle(0, 10)
+    mlp(1, SERVE[1], lambda: finish_out(0), lambda: forward(0, 14, out_at))
+    sent(1, 0)
+    for k in range(2):
+        act_msg(1, k).wait_recv()
+    product(1, act[...], wd_v, {}, 10, True)
+    rs_middle(1, 10)
+    arrive(0, 14, out_at)
+    finish_out(1)
+    forward(1, 14, out_at)
+    gates_sent(1)
+    for c in range(CHUNKS):
+        sent(c, 4, mid_at)
+        sent(c, 10)
+        if c == 0:
+            sent(c, 14, out_at)
+    for k in range(2):
+        act_msg(1, k).wait_send()
     attn_msg.wait_send()
+    arrive(1, 14, out_at)
+    sent(1, 14, out_at)
 
 
 def tail(attn, x_in, gain, w_o, w_gate, w_up, w_down):
@@ -454,8 +484,8 @@
         scratch_shapes=[
             pltpu.VMEM((2, rows // 2, q_width), bf16),
             pltpu.VMEM((rows, PIECE), bf16),
-            pltpu.VMEM((4, q_width, PIECE), bf16),
-            pltpu.VMEM((4, ff, PIECE), bf16),
+            pltpu.VMEM((q_width, hidden), bf16),
+            pltpu.VMEM((ff, hidden), bf16),
             pltpu.VMEM((RING, hidden, 2 * TILE), bf16),
             pltpu.VMEM((CHUNKS, 2, 3, sub, PIECE), bf16),
             pltpu.VMEM((CHUNKS, 2, 3, sub, PIECE), bf16),
@@ -468,7 +498,7 @@
             pltpu.VMEM((CHUNKS, 2 * sub, 128), f32),
             pltpu.VMEM((CHUNKS, 2 * sub, 128), f32),
             dma((4,)), dma((4,)), dma((RING, 2)), dma(()),
-            dma((CHUNKS, 2, 12)), dma((CHUNKS, 2, 12)),
+            dma((CHUNKS, 2, 20)), dma((CHUNKS, 2, 20)),
             dma((CHUNKS, steps)), dma((CHUNKS, steps)),
             dma((CHUNKS, 2)), dma((CHUNKS, 2)),
             dma((CHUNKS,)), dma((CHUNKS,)),
@@ -479,8 +509,8 @@
     )(attn, x_in, gain, w_o, w_gate, w_up, w_down)
 
 
-def head_kernel(x_hbm, gain_ref, bq_ref, bk_ref, bv_ref, cos_ref, sin_ref, wq_hbm, wk_hbm, wv_hbm, q_out, k_out, v_out,
-                xv, wv_all, hbuf, keep, psend, precv, ssq, ssr, x_sem, w_sem, st_ss, st_rs, p_ss, p_rs):
+def head_kernel(lens, x_hbm, gain_ref, bq_ref, bk_ref, bv_ref, freq_ref, wq_hbm, wk_hbm, wv_hbm, q_out, k_out, v_out,
+                xv, wv_all, hbuf, keep, psend, precv, ssq, ssr, cos_ref, sin_ref, x_sem, w_sem, st_ss, st_rs, p_ss, p_rs):
     my, mx = lax.axis_index("my"), lax.axis_index("mx")
     rows, hidden = xv.shape
     half = rows // 2
@@ -507,10 +537,10 @@
     for i in range(x_parts):
         x_copies[i].wait()
 
-        @pl.loop(0, x_rows // ROWS_STEP)
+        @pl.loop(0, x_rows // HEAD_ROWS)
         def _(step, i=i):
-            at = pl.ds(pl.multiple_of(i * x_rows + step * ROWS_STEP, ROWS_STEP), ROWS_STEP)
-            total = jnp.zeros((ROWS_STEP, 128), jnp.float32)
+            at = pl.ds(pl.multiple_of(i * x_rows + step * HEAD_ROWS, HEAD_ROWS), HEAD_ROWS)
+            total = jnp.zeros((HEAD_ROWS, 128), jnp.float32)
             for k in range(0, hidden, 128):
                 m = xv[at, k:k + 128].astype(jnp.float32)
                 total = total + m * m
@@ -518,12 +548,26 @@
     pl.semaphore_wait(barrier, 1)
     stats = remote(ssq, ssr, st_ss, st_rs)
     stats.start()
+    row_of = lax.broadcasted_iota(jnp.int32, (ROWS_STEP, HEAD), 0)
+    lower = lax.broadcasted_iota(jnp.int32, (ROWS_STEP, HEAD), 1) < HEAD // 2
+
+    @pl.loop(0, half // ROWS_STEP)
+    def _(step):
+        start = pl.multiple_of(step * ROWS_STEP, ROWS_STEP)
+        pos = jnp.zeros((ROWS_STEP, HEAD), jnp.int32)
+        for i in range(ROWS_STEP):
+            pos = jnp.where(row_of == i, lens[start + i], pos)
+        angles = pos.astype(jnp.float32) * freq_ref[0:1, :]
+        cos_ref[pl.ds(start, ROWS_STEP), :] = jnp.cos(angles)
+        sin = jnp.sin(angles)
+        sin_ref[pl.ds(start, ROWS_STEP), :] = jnp.where(lower, -sin, sin)
+
     stats.wait()
 
     def normalise(start):
-        @pl.loop(0, half // ROWS_STEP)
+        @pl.loop(0, half // NORM_ROWS)
         def _(step):
-            at = pl.ds(pl.multiple_of(start + step * ROWS_STEP, ROWS_STEP), ROWS_STEP)
+            at = pl.ds(pl.multiple_of(start + step * NORM_ROWS, NORM_ROWS), NORM_ROWS)
             total = jnp.sum(ssq[at, :] + ssr[at, :], axis=1, keepdims=True)
             inv = lax.rsqrt(total / (2 * hidden) + NORM_EPS)
             for k in range(hidden // 128):
@@ -574,7 +618,7 @@
         piece(i, lo, hi).wait_send()
 
 
-def head(x_in, gain, b_q, b_k, b_v, cos_tab, sin_tab, w_q, w_k, w_v):
+def head(lens, x_in, gain, b_q, b_k, b_v, freq, w_q, w_k, w_v):
     rows, hidden = x_in.shape
     half = rows // 2
     q_cols, kv_cols = w_q.shape[1], w_k.shape[1]
@@ -586,7 +630,7 @@
     return pl.pallas_call(
         head_kernel,
         out_shape=(jax.ShapeDtypeStruct((half, q_cols), f32), jax.ShapeDtypeStruct((half, kv_cols), f32), jax.ShapeDtypeStruct((half, kv_cols), f32)),
-        in_specs=[hbm] + [whole] * 6 + [hbm] * 3,
+        in_specs=[pl.BlockSpec(memory_space=pltpu.SMEM), hbm] + [whole] * 5 + [hbm] * 3,
         out_specs=(whole, whole, whole),
         scratch_shapes=[
             pltpu.VMEM((rows, hidden), bf16),
@@ -597,11 +641,13 @@
             pltpu.VMEM((half, width), bf16),
             pltpu.VMEM((rows, 128), f32),
             pltpu.VMEM((rows, 128), f32),
+            pltpu.VMEM((half, HEAD), f32),
+            pltpu.VMEM((half, HEAD), f32),
             dma((4,)), dma((3,)), dma(()), dma(()), dma((4,)), dma((4,)),
         ],
         compiler_params=pltpu.CompilerParams(collective_id=0, has_side_effects=True, vmem_limit_bytes=67043328),
         name="head",
-    )(x_in, gain, b_q, b_k, b_v, cos_tab, sin_tab, w_q, w_k, w_v)
+    )(lens, x_in, gain, b_q, b_k, b_v, freq, w_q, w_k, w_v)
 
 
 def lanes_of(vec):
@@ -617,10 +663,8 @@
     def local_layer(x_in, seq_lens, gain_attn, gain_mlp, w_q, b_q, w_k, b_k, w_v, b_v, w_o, w_gate, w_up, w_down, k_cache, v_cache):
         half_dim = HEAD // 2
         inv_freq = (ROPE_THETA ** (-2.0 * (np.arange(HEAD) % half_dim) / HEAD)).astype(np.float32)
-        sign = np.where(np.arange(HEAD) < half_dim, -1.0, 1.0).astype(np.float32)
-        angles = seq_lens.astype(jnp.float32)[:, None] * inv_freq
-        cos_tab, sin_tab = jnp.cos(angles), jnp.sin(angles) * sign
-        q_rot, k_rot, v_new = head(x_in, lanes_of(gain_attn), lanes_of(b_q), lanes_of(b_k), lanes_of(b_v), cos_tab, sin_tab, w_q, w_k, w_v)
+        freq = jnp.asarray(np.broadcast_to(inv_freq, (8, HEAD)))
+        q_rot, k_rot, v_new = head(seq_lens, x_in, lanes_of(gain_attn), lanes_of(b_q), lanes_of(b_k), lanes_of(b_v), freq, w_q, w_k, w_v)
         k_cache_out, v_cache_out, attn_rows = attend(seq_lens, q_rot, k_rot, v_new, k_cache, v_cache)
         x_out = tail(attn_rows, x_in, lanes_of(gain_mlp), w_o, w_gate, w_up, w_down)
         return x_out, k_cache_out, v_cache_out

time: 166 us -> 142 us (0.86)
  Pallas kernels: 160 us -> 137 us
  other arithmetic: 2.46 us -> 0 us
    pallas_call x1, Pallas kernels: 107 us -> 85.7 us  [tail(): pl.pallas_call(tail_kernel, out_shape=jax.ShapeDtypeStruct((rows, hidden)...]
    pallas_call x1, Pallas kernels: 16.7 us -> 14.9 us  [head(): pl.pallas_call(head_kernel, out_shape=(jax.ShapeDtypeStruct((half, q_cols...]
    mul x1 -> x0, other arithmetic: 1.77 us -> none  [local_layer(): cos_tab, sin_tab = (jnp.cos(angles), jnp.sin(angles) * sign)]
where the time goes in v4:
time: 142 us
  Pallas kernels  137 us (96%)
  local copies, waits for them, and re-layouts  4.2 us (3%)
    pallas_call x1, Pallas kernels, tail(): pl.pallas_call(tail_kernel, out_shape=jax.ShapeDtypeStruct((rows, hidden)...  85.7 us
    pallas_call x1, Pallas kernels, attend(): pl.pallas_call(attend_kernel, out_shape=(jax.ShapeDtypeStruct(kc.shape, k...  36.1 us
    pallas_call x1, Pallas kernels, head(): pl.pallas_call(head_kernel, out_shape=(jax.ShapeDtypeStruct((half, q_cols...  14.9 us
    unnamed x1, local copies, waits for them, and re-layouts  2.94 us

profile of v4, /device:TPU:0, one launch (start us, length us, event | category | flops | bytes accessed | tf_op | source)
XLA Modules:
  0.0 141.6 jit_solution(11524477187302057995)
XLA Ops:
  0.6 1.3 jit_solution_.3.freq_ref
  1.9 14.9 %head.1 = (f32[192,1280]{1,0:T(8,128)}, f32[192,256]{1,0:T(8,128)}, f32[192,256]{1,0:T(8,128)}) custom-call(s32[192]{0:T(256)} %lens.3, bf16[384,2560]{1,0:T(8,128)(2,1)} %x_hbm.3, bf16[20,128]{1,0:T(8,128)(2,1)} %bitcast.11, bf16[10,128]{1,0:T(8,128)(2,1)} %bitcast.13, bf16[2,128]{1,0:T(2,128)(2,1)} %bitcast.14, bf16[2,128]{1,0:T(2,128)(2,1)} %bitcast.15, ...), custom_call_target="tpu_custom_call" | custom-call | tf_op jit(solution)/shard_map/head/pallas_call | solution.py:630
  16.8 36.1 %attend.1 = (bf16[192,512,128]{2,1,0:T(8,128)(2,1)}, bf16[192,512,128]{2,1,0:T(8,128)(2,1)}, bf16[192,1280]{1,0:T(8,128)(2,1)}) custom-call(s32[192]{0:T(256)} %lens.3, f32[192,1280]{1,0:T(8,128)} %get-tuple-element.9.q_hbm, f32[192,256]{1,0:T(8,128)} %get-tuple-element.10.kn_hbm, f32[192,256]{1,0:T(8,128)} %get-tuple-element.11.vn_hbm, ...), custom_call_target="tpu_custom_call" | custom-call | tf_op jit(solution)/shard_map/attend/pallas_call | solution.py:143
  52.9 85.7 %tail.1 = bf16[384,2560]{1,0:T(8,128)(2,1)} custom-call(bf16[192,1280]{1,0:T(8,128)(2,1)} %get-tuple-element.12.attn_hbm, bf16[384,2560]{1,0:T(8,128)(2,1)} %x_hbm.3, bf16[20,128]{1,0:T(8,128)(2,1)} %bitcast.12, bf16[1280,2560]{1,0:T(8,128)(2,1)} %wo_hbm.1, bf16[2560,3456]{1,0:T(8,128)(2,1)} %wg_hbm.1, bf16[2560,3456]{1,0:T(8,128)(2,1)} %wu_hbm.1, ...), custom_call_target="tpu_custom_call" | custom-call | tf_op jit(solution)/shard_map/tail/pallas_call | solution.py:479
  138.6 2.9 %copy.21 = bf16[384,2560]{1,0:T(8,128)(2,1)} copy(bf16[384,2560]{1,0:T(8,128)(2,1)} %tail.1) | data formatting | bytes 3932160

commit v5 on v4

--- a/solution.py
+++ b/solution.py
@@ -1,6 +1,7 @@
+import math
+
 import jax
 import jax.numpy as jnp
-import numpy as np
 from jax import lax
 from jax.experimental import pallas as pl
 from jax.experimental.pallas import tpu as pltpu
@@ -24,7 +25,7 @@
 MESH = pl.DeviceIdType.MESH
 
 
-def attend_kernel(lens, q_hbm, kn_hbm, vn_hbm, kc, vc, ko, vo, out_hbm, kbuf, vbuf, q_ref, kn_ref, vn_ref, out_ref, qs, os, sems, in_sem, out_sem):
+def attend_kernel(lens_hbm, q_hbm, kn_hbm, vn_hbm, kc, vc, ko, vo, out_hbm, kbuf, vbuf, q_ref, kn_ref, vn_ref, out_ref, qs, os, sems, in_sem, out_sem, lens):
     rows = q_ref.shape[0]
     heads = q_ref.shape[1] // HEAD
     flat = kbuf.shape[2]
@@ -38,12 +39,12 @@
         return (pltpu.make_async_copy(kbuf.at[slot], ko.at[part], sems.at[2, slot]),
                 pltpu.make_async_copy(vbuf.at[slot], vo.at[part], sems.at[3, slot]))
 
+    loads = [pltpu.make_async_copy(src, dst, in_sem.at[i]) for i, (src, dst) in enumerate(((lens_hbm, lens), (q_hbm, q_ref), (kn_hbm, kn_ref), (vn_hbm, vn_ref)))]
+    for load in loads:
+        load.start()
     for block in range(AHEAD):
         for move in moves(block, block, True):
             move.start()
-    loads = [pltpu.make_async_copy(src, dst, in_sem.at[i]) for i, (src, dst) in enumerate(((q_hbm, q_ref), (kn_hbm, kn_ref), (vn_hbm, vn_ref)))]
-    for load in loads:
-        load.start()
     qs[...] = jnp.zeros_like(qs)
 
     def put_out(step):
@@ -143,7 +144,7 @@
     ko, vo, out = pl.pallas_call(
         attend_kernel,
         out_shape=(jax.ShapeDtypeStruct(kc.shape, kc.dtype), jax.ShapeDtypeStruct(vc.shape, vc.dtype), jax.ShapeDtypeStruct(q.shape, jnp.bfloat16)),
-        in_specs=[pl.BlockSpec(memory_space=pltpu.SMEM)] + [hbm] * 5,
+        in_specs=[hbm] * 6,
         out_specs=(hbm, hbm, hbm),
         scratch_shapes=[
             pltpu.VMEM((SLOTS, SLOT_ROWS, flat, HEAD), jnp.bfloat16),
@@ -155,8 +156,9 @@
             pltpu.VMEM((SLOT_ROWS * PAD_HEADS, HEAD), jnp.float32),
             pltpu.VMEM((2 * SLOT_ROWS * PAD_HEADS, HEAD), jnp.float32),
             pltpu.SemaphoreType.DMA((4, SLOTS)),
-            pltpu.SemaphoreType.DMA((3,)),
+            pltpu.SemaphoreType.DMA((4,)),
             pltpu.SemaphoreType.DMA(()),
+            pltpu.SMEM(lens.shape, lens.dtype),
         ],
         compiler_params=pltpu.CompilerParams(vmem_limit_bytes=67043328),
         name="attend",
@@ -164,9 +166,9 @@
     return ko.reshape(k_cache.shape), vo.reshape(v_cache.shape), out
 
 
-def tail_kernel(attn_hbm, x_hbm, gain_ref, wo_hbm, wg_hbm, wu_hbm, wd_hbm, out_ref,
+def tail_kernel(attn_hbm, x_hbm, gain_hbm, wo_hbm, wg_hbm, wu_hbm, wd_hbm, out_ref,
                 attn_all, xown, wo_v, wd_v, ring, sb, rb, keep, mall, hbuf, gsend, grecv, act, ssq, ssr,
-                wo_sem, wd_sem, ring_sem, x_sem, ici_ss, ici_rs, gu_ss, gu_rs, act_ss, act_rs, st_ss, st_rs, at_ss, at_rs, at_sem):
+                wo_sem, wd_sem, ring_sem, x_sem, ici_ss, ici_rs, gu_ss, gu_rs, act_ss, act_rs, st_ss, st_rs, at_ss, at_rs, at_sem, gain_ref, gain_sem):
     my, mx = lax.axis_index("my"), lax.axis_index("mx")
     row_count, hidden = out_ref.shape
     half_rows = row_count // 2
@@ -204,6 +206,8 @@
     for r in order:
         wo_copies[r].start()
     x_copy.start()
+    gain_copy = pltpu.make_async_copy(gain_hbm, gain_ref, gain_sem)
+    gain_copy.start()
 
     def ring_copies(g):
         slot = lax.rem(g, RING)
@@ -421,6 +425,7 @@
             copy.start()
     product(1, attn_lhs(1), wo_v, {}, 0, False)
     x_copy.wait()
+    gain_copy.wait()
     for r in order:
         wd_copies[r].start()
     rs_middle(0, 0)
@@ -479,7 +484,7 @@
     return pl.pallas_call(
         tail_kernel,
         out_shape=jax.ShapeDtypeStruct((rows, hidden), bf16),
-        in_specs=[hbm, hbm, whole, hbm, hbm, hbm, hbm],
+        in_specs=[hbm] * 7,
         out_specs=whole,
         scratch_shapes=[
             pltpu.VMEM((2, rows // 2, q_width), bf16),
@@ -503,14 +508,15 @@
             dma((CHUNKS, 2)), dma((CHUNKS, 2)),
             dma((CHUNKS,)), dma((CHUNKS,)),
             dma(()), dma(()), dma(()),
+            pltpu.VMEM(gain.shape, bf16), dma(()),
         ],
         compiler_params=pltpu.CompilerParams(collective_id=1, has_side_effects=True, vmem_limit_bytes=67043328),
         name="tail",
     )(attn, x_in, gain, w_o, w_gate, w_up, w_down)
 
 
-def head_kernel(lens, x_hbm, gain_ref, bq_ref, bk_ref, bv_ref, freq_ref, wq_hbm, wk_hbm, wv_hbm, q_out, k_out, v_out,
-                xv, wv_all, hbuf, keep, psend, precv, ssq, ssr, cos_ref, sin_ref, x_sem, w_sem, st_ss, st_rs, p_ss, p_rs):
+def head_kernel(lens_hbm, x_hbm, gain_hbm, bq_hbm, bk_hbm, bv_hbm, wq_hbm, wk_hbm, wv_hbm, q_out, k_out, v_out,
+                xv, wv_all, hbuf, keep, psend, precv, ssq, ssr, cos_ref, sin_ref, x_sem, w_sem, st_ss, st_rs, p_ss, p_rs, lens, gain_ref, bq_ref, bk_ref, bv_ref, small_sem):
     my, mx = lax.axis_index("my"), lax.axis_index("mx")
     rows, hidden = xv.shape
     half = rows // 2
@@ -528,7 +534,8 @@
         pltpu.make_async_copy(wk_hbm, wv_all.at[:, pl.ds(q_cols, kv_cols)], w_sem.at[1]),
         pltpu.make_async_copy(wv_hbm, wv_all.at[:, pl.ds(q_cols + kv_cols, kv_cols)], w_sem.at[2]),
     ]
-    for copy in x_copies + w_copies:
+    small = [pltpu.make_async_copy(src, dst, small_sem.at[i]) for i, (src, dst) in enumerate(((lens_hbm, lens), (gain_hbm, gain_ref), (bq_hbm, bq_ref), (bk_hbm, bk_ref), (bv_hbm, bv_ref)))]
+    for copy in x_copies + small + w_copies:
         copy.start()
 
     def remote(src, dst, ss, rs):
@@ -548,8 +555,12 @@
     pl.semaphore_wait(barrier, 1)
     stats = remote(ssq, ssr, st_ss, st_rs)
     stats.start()
+    for copy in small:
+        copy.wait()
     row_of = lax.broadcasted_iota(jnp.int32, (ROWS_STEP, HEAD), 0)
-    lower = lax.broadcasted_iota(jnp.int32, (ROWS_STEP, HEAD), 1) < HEAD // 2
+    lane = lax.broadcasted_iota(jnp.int32, (ROWS_STEP, HEAD), 1)
+    lower = lane < HEAD // 2
+    freq = jnp.exp(lax.rem(lane, HEAD // 2).astype(jnp.float32) * (-2.0 * math.log(ROPE_THETA) / HEAD))
 
     @pl.loop(0, half // ROWS_STEP)
     def _(step):
@@ -557,7 +568,7 @@
         pos = jnp.zeros((ROWS_STEP, HEAD), jnp.int32)
         for i in range(ROWS_STEP):
             pos = jnp.where(row_of == i, lens[start + i], pos)
-        angles = pos.astype(jnp.float32) * freq_ref[0:1, :]
+        angles = pos.astype(jnp.float32) * freq
         cos_ref[pl.ds(start, ROWS_STEP), :] = jnp.cos(angles)
         sin = jnp.sin(angles)
         sin_ref[pl.ds(start, ROWS_STEP), :] = jnp.where(lower, -sin, sin)
@@ -618,7 +629,7 @@
         piece(i, lo, hi).wait_send()
 
 
-def head(lens, x_in, gain, b_q, b_k, b_v, freq, w_q, w_k, w_v):
+def head(lens, x_in, gain, b_q, b_k, b_v, w_q, w_k, w_v):
     rows, hidden = x_in.shape
     half = rows // 2
     q_cols, kv_cols = w_q.shape[1], w_k.shape[1]
@@ -630,7 +641,7 @@
     return pl.pallas_call(
         head_kernel,
         out_shape=(jax.ShapeDtypeStruct((half, q_cols), f32), jax.ShapeDtypeStruct((half, kv_cols), f32), jax.ShapeDtypeStruct((half, kv_cols), f32)),
-        in_specs=[pl.BlockSpec(memory_space=pltpu.SMEM), hbm] + [whole] * 5 + [hbm] * 3,
+        in_specs=[hbm] * 9,
         out_specs=(whole, whole, whole),
         scratch_shapes=[
             pltpu.VMEM((rows, hidden), bf16),
@@ -644,10 +655,13 @@
             pltpu.VMEM((half, HEAD), f32),
             pltpu.VMEM((half, HEAD), f32),
             dma((4,)), dma((3,)), dma(()), dma(()), dma((4,)), dma((4,)),
+            pltpu.SMEM(lens.shape, lens.dtype),
+            pltpu.VMEM(gain.shape, bf16), pltpu.VMEM(b_q.shape, bf16), pltpu.VMEM(b_k.shape, bf16), pltpu.VMEM(b_v.shape, bf16),
+            dma((5,)),
         ],
         compiler_params=pltpu.CompilerParams(collective_id=0, has_side_effects=True, vmem_limit_bytes=67043328),
         name="head",
-    )(lens, x_in, gain, b_q, b_k, b_v, freq, w_q, w_k, w_v)
+    )(lens, x_in, gain, b_q, b_k, b_v, w_q, w_k, w_v)
 
 
 def lanes_of(vec):
@@ -661,10 +675,7 @@
     out_specs = (act_spec, cache_spec, cache_spec)
 
     def local_layer(x_in, seq_lens, gain_attn, gain_mlp, w_q, b_q, w_k, b_k, w_v, b_v, w_o, w_gate, w_up, w_down, k_cache, v_cache):
-        half_dim = HEAD // 2
-        inv_freq = (ROPE_THETA ** (-2.0 * (np.arange(HEAD) % half_dim) / HEAD)).astype(np.float32)
-        freq = jnp.asarray(np.broadcast_to(inv_freq, (8, HEAD)))
-        q_rot, k_rot, v_new = head(seq_lens, x_in, lanes_of(gain_attn), lanes_of(b_q), lanes_of(b_k), lanes_of(b_v), freq, w_q, w_k, w_v)
+        q_rot, k_rot, v_new = head(seq_lens, x_in, lanes_of(gain_attn), lanes_of(b_q), lanes_of(b_k), lanes_of(b_v), w_q, w_k, w_v)
         k_cache_out, v_cache_out, attn_rows = attend(seq_lens, q_rot, k_rot, v_new, k_cache, v_cache)
         x_out = tail(attn_rows, x_in, lanes_of(gain_mlp), w_o, w_gate, w_up, w_down)
         return x_out, k_cache_out, v_cache_out

time: 142 us -> 137 us (0.965)
  Pallas kernels: 137 us -> 134 us
    pallas_call x1, Pallas kernels: 36.1 us -> 34.6 us  [attend(): pl.pallas_call(attend_kernel, out_shape=(jax.ShapeDtypeStruct(kc.shape, k...]
where the time goes in v5:
time: 137 us
  Pallas kernels  134 us (98%)
  local copies, waits for them, and re-layouts  2.94 us (2%)
    pallas_call x1, Pallas kernels, tail(): pl.pallas_call(tail_kernel, out_shape=jax.ShapeDtypeStruct((rows, hidden)...  85.1 us
    pallas_call x1, Pallas kernels, attend(): pl.pallas_call(attend_kernel, out_shape=(jax.ShapeDtypeStruct(kc.shape, k...  34.6 us
    pallas_call x1, Pallas kernels, head(): pl.pallas_call(head_kernel, out_shape=(jax.ShapeDtypeStruct((half, q_cols...  14.1 us
    unnamed x1, local copies, waits for them, and re-layouts  2.94 us

profile of v5, /device:TPU:0, one launch (start us, length us, event | category | flops | bytes accessed | tf_op | source)
XLA Modules:
  0.0 137.3 jit_solution(9140385879641914753)
XLA Ops:
  0.6 14.1 %head.1 = (f32[192,1280]{1,0:T(8,128)}, f32[192,256]{1,0:T(8,128)}, f32[192,256]{1,0:T(8,128)}) custom-call(s32[192]{0:T(256)} %lens_hbm.3, bf16[384,2560]{1,0:T(8,128)(2,1)} %x_hbm.3, bf16[20,128]{1,0:T(8,128)(2,1)} %bitcast.11, bf16[10,128]{1,0:T(8,128)(2,1)} %bitcast.13, bf16[2,128]{1,0:T(2,128)(2,1)} %bitcast.14, bf16[2,128]{1,0:T(2,128)(2,1)} %bitcast.15, ...), custom_call_target="tpu_custom_call" | custom-call | tf_op jit(solution)/shard_map/head/pallas_call | solution.py:641
  14.8 34.6 %attend.1 = (bf16[192,512,128]{2,1,0:T(8,128)(2,1)}, bf16[192,512,128]{2,1,0:T(8,128)(2,1)}, bf16[192,1280]{1,0:T(8,128)(2,1)}) custom-call(s32[192]{0:T(256)} %lens_hbm.3, f32[192,1280]{1,0:T(8,128)} %get-tuple-element.9.q_hbm, f32[192,256]{1,0:T(8,128)} %get-tuple-element.10.kn_hbm, f32[192,256]{1,0:T(8,128)} %get-tuple-element.11.vn_hbm, ...), custom_call_target="tpu_custom_call" | custom-call | tf_op jit(solution)/shard_map/attend/pallas_call | solution.py:144
  49.3 85.1 %tail.1 = bf16[384,2560]{1,0:T(8,128)(2,1)} custom-call(bf16[192,1280]{1,0:T(8,128)(2,1)} %get-tuple-element.12.attn_hbm, bf16[384,2560]{1,0:T(8,128)(2,1)} %x_hbm.3, bf16[20,128]{1,0:T(8,128)(2,1)} %bitcast.12, bf16[1280,2560]{1,0:T(8,128)(2,1)} %wo_hbm.1, bf16[2560,3456]{1,0:T(8,128)(2,1)} %wg_hbm.1, bf16[2560,3456]{1,0:T(8,128)(2,1)} %wu_hbm.1, ...), custom_call_target="tpu_custom_call" | custom-call | tf_op jit(solution)/shard_map/tail/pallas_call | solution.py:484
  134.4 2.9 %copy.20 = bf16[384,2560]{1,0:T(8,128)(2,1)} copy(bf16[384,2560]{1,0:T(8,128)(2,1)} %tail.1) | data formatting | bytes 3932160

commit v6 on v5

--- a/solution.py
+++ b/solution.py
@@ -20,7 +20,7 @@
 TILE = 256
 ROWS_STEP = 16
 NORM_ROWS = 64
-SERVE = ((5, 11), (9, 14))
+SERVE = ((5, 11), (7, 13))
 HEAD_ROWS = 48
 MESH = pl.DeviceIdType.MESH
 
@@ -535,7 +535,7 @@
         pltpu.make_async_copy(wv_hbm, wv_all.at[:, pl.ds(q_cols + kv_cols, kv_cols)], w_sem.at[2]),
     ]
     small = [pltpu.make_async_copy(src, dst, small_sem.at[i]) for i, (src, dst) in enumerate(((lens_hbm, lens), (gain_hbm, gain_ref), (bq_hbm, bq_ref), (bk_hbm, bk_ref), (bv_hbm, bv_ref)))]
-    for copy in x_copies + small + w_copies:
+    for copy in x_copies + small:
         copy.start()
 
     def remote(src, dst, ss, rs):
@@ -543,6 +543,9 @@
 
     for i in range(x_parts):
         x_copies[i].wait()
+        if i == x_parts - 1:
+            for copy in w_copies:
+                copy.start()
 
         @pl.loop(0, x_rows // HEAD_ROWS)
         def _(step, i=i):

time: 137 us -> 136 us (level)
  Pallas kernels: 134 us -> 132 us
where the time goes in v6:
time: 136 us
  Pallas kernels  132 us (97%)
  local copies, waits for them, and re-layouts  2.94 us (2%)
    pallas_call x1, Pallas kernels, tail(): pl.pallas_call(tail_kernel, out_shape=jax.ShapeDtypeStruct((rows, hidden)...  84.7 us
    pallas_call x1, Pallas kernels, attend(): pl.pallas_call(attend_kernel, out_shape=(jax.ShapeDtypeStruct(kc.shape, k...  34.6 us
    pallas_call x1, Pallas kernels, head(): pl.pallas_call(head_kernel, out_shape=(jax.ShapeDtypeStruct((half, q_cols...  13.1 us
    unnamed x1, local copies, waits for them, and re-layouts  2.94 us

profile of v6, /device:TPU:0, one launch (start us, length us, event | category | flops | bytes accessed | tf_op | source)
XLA Modules:
  0.0 135.9 jit_solution(7755719384921481079)
XLA Ops:
  0.6 13.1 %head.1 = (f32[192,1280]{1,0:T(8,128)}, f32[192,256]{1,0:T(8,128)}, f32[192,256]{1,0:T(8,128)}) custom-call(s32[192]{0:T(256)} %lens_hbm.3, bf16[384,2560]{1,0:T(8,128)(2,1)} %x_hbm.3, bf16[20,128]{1,0:T(8,128)(2,1)} %bitcast.11, bf16[10,128]{1,0:T(8,128)(2,1)} %bitcast.13, bf16[2,128]{1,0:T(2,128)(2,1)} %bitcast.14, bf16[2,128]{1,0:T(2,128)(2,1)} %bitcast.15, ...), custom_call_target="tpu_custom_call" | custom-call | tf_op jit(solution)/shard_map/head/pallas_call | solution.py:644
  13.7 34.6 %attend.1 = (bf16[192,512,128]{2,1,0:T(8,128)(2,1)}, bf16[192,512,128]{2,1,0:T(8,128)(2,1)}, bf16[192,1280]{1,0:T(8,128)(2,1)}) custom-call(s32[192]{0:T(256)} %lens_hbm.3, f32[192,1280]{1,0:T(8,128)} %get-tuple-element.9.q_hbm, f32[192,256]{1,0:T(8,128)} %get-tuple-element.10.kn_hbm, f32[192,256]{1,0:T(8,128)} %get-tuple-element.11.vn_hbm, ...), custom_call_target="tpu_custom_call" | custom-call | tf_op jit(solution)/shard_map/attend/pallas_call | solution.py:144
  48.3 84.7 %tail.1 = bf16[384,2560]{1,0:T(8,128)(2,1)} custom-call(bf16[192,1280]{1,0:T(8,128)(2,1)} %get-tuple-element.12.attn_hbm, bf16[384,2560]{1,0:T(8,128)(2,1)} %x_hbm.3, bf16[20,128]{1,0:T(8,128)(2,1)} %bitcast.12, bf16[1280,2560]{1,0:T(8,128)(2,1)} %wo_hbm.1, bf16[2560,3456]{1,0:T(8,128)(2,1)} %wg_hbm.1, bf16[2560,3456]{1,0:T(8,128)(2,1)} %wu_hbm.1, ...), custom_call_target="tpu_custom_call" | custom-call | tf_op jit(solution)/shard_map/tail/pallas_call | solution.py:484
  133.0 2.9 %copy.20 = bf16[384,2560]{1,0:T(8,128)(2,1)} copy(bf16[384,2560]{1,0:T(8,128)(2,1)} %tail.1) | data formatting | bytes 3932160
